TPU v7x, 32 devices: a whole 2x2x4 slice. The times are simulated.
32 devices in a mesh: section: 2 (over core), shard: 4 (over z), rep: 4 (over y, x).
Axes of the slice: x: 2, y: 2, z: 4, core: 2. Of those that a mesh axis runs over, the one named last changes fastest.
Arguments:
- boundary: bfloat16 [2, 2, 16, 256, 1536], P('section', None, ('shard', 'rep')), may hold values from -6 to 6
- lengths: int32 [2, 16], P(None, ('shard', 'rep')), may hold values from 1 to 256, 2457 in all within a row
- in_proj: bfloat16 [2, 1536, 6400], P('section', 'shard'), may hold values from -0.15625 to 0.15625
- dt_proj: bfloat16 [2, 1536, 48], P('section', 'shard'), may hold values from -0.15625 to 0.15625
- out_proj: bfloat16 [2, 3072, 1536], P('section', 'shard'), may hold values from -0.109375 to 0.109375
- conv_weight: bfloat16 [2, 4, 3328], P('section', None, 'shard'), may hold values from -3 to 3
- conv_bias: bfloat16 [2, 3328], P('section', 'shard'), may hold values from -3 to 3
- dt_bias: bfloat16 [2, 48], P('section', 'shard'), may hold values from -6 to -2
- a_log: bfloat16 [2, 48], P('section', 'shard'), may hold values from 0 to 2.765625
- d_skip: bfloat16 [2, 48], P('section', 'shard'), may hold values from 0.5 to 1.5
- pre_gain: bfloat16 [2, 1536], P('section', 'shard'), may hold values from 0.5 to 1.5
- out_gain: bfloat16 [2, 3072], P('section', 'shard'), may hold values from 0.5 to 1.5
Outputs:
- activations: bfloat16 [2, 2, 16, 256, 1536], P('section', None, ('shard', 'rep'))
- input_grads: bfloat16 [2, 2, 16, 256, 1536], P('section', None, ('shard', 'rep'))
- grad_in_proj: float32 [2, 1536, 6400], P('section', 'shard')
- grad_dt_proj: float32 [2, 1536, 48], P('section', 'shard')
- grad_out_proj: float32 [2, 3072, 1536], P('section', 'shard')
- grad_conv_weight: float32 [2, 4, 3328], P('section', None, 'shard')
- grad_conv_bias: float32 [2, 3328], P('section', 'shard')
- grad_dt_bias: float32 [2, 48], P('section', 'shard')
- grad_a_log: float32 [2, 48], P('section', 'shard')
- grad_d_skip: float32 [2, 48], P('section', 'shard')
- grad_pre_gain: float32 [2, 1536], P('section', 'shard')
- grad_out_gain: float32 [2, 3072], P('section', 'shard')
Inputs may be any that keep to these rules, and one draw needn't show every extreme that they name: `lengths`: in each micro-batch some sequence has exactly 256 tokens.
All inputs are finite; a program needn't handle non-finite values. No bound on the sum of `lengths` on one device may be relied on, other than what follows from the above.
Results may differ from a plain program's by a relative error of at most 0.02.
Values may be sent and summed in bfloat16 or wider, within the bound.
A program may use at most 768 MiB of HBM per device.

v0:
```python
import functools

import jax
import jax.numpy as jnp
from jax import lax
from jax.experimental import pallas as pl
from jax.experimental.pallas import tpu as pltpu
from jax.sharding import PartitionSpec as P


BF = jnp.bfloat16
F32 = jnp.float32
HIGH = lax.Precision.HIGHEST
EPSILON = 1e-05
CHUNK = 128
LANES = 128
PAIR = 2


def mm(a, b):
    return jnp.dot(a.astype(BF), b.astype(BF), preferred_element_type=F32)


def mm_t(a, b):
    return lax.dot_general(a.astype(BF), b.astype(BF), (((1,), (1,)), ((), ())), preferred_element_type=F32)


def t_mm(a, b):
    return lax.dot_general(a.astype(BF), b.astype(BF), (((0,), (0,)), ((), ())), preferred_element_type=F32)


def rows_of(shape):
    return lax.broadcasted_iota(jnp.int32, shape, 0)


def lanes_of(shape):
    return lax.broadcasted_iota(jnp.int32, shape, 1)


def shift_down(v, steps):
    return jnp.where(rows_of(v.shape) >= steps, pltpu.roll(v, steps, 0), 0.0)


def shift_up(v, steps):
    size = v.shape[0]
    return jnp.where(rows_of(v.shape) < size - steps, pltpu.roll(v, size - steps, 0), 0.0)


def conv(v, taps_ref, taps):
    total = taps_ref[taps : taps + 1, :] + taps_ref[taps - 1 : taps, :] * v
    for k in range(taps - 1):
        total = total + taps_ref[k : k + 1, :] * shift_down(v, taps - 1 - k)
    return total


def conv_back(d_sum, v, taps_ref, taps):
    d_v = taps_ref[taps - 1 : taps, :] * d_sum
    d_taps = []
    for k in range(taps - 1):
        d_v = d_v + taps_ref[k : k + 1, :] * shift_up(d_sum, taps - 1 - k)
        d_taps.append(jnp.sum(d_sum * shift_down(v, taps - 1 - k), axis=0, keepdims=True))
    d_taps.append(jnp.sum(d_sum * v, axis=0, keepdims=True))
    d_taps.append(jnp.sum(d_sum, axis=0, keepdims=True))
    return d_v, d_taps


def head_map(width, head_dim):
    shape = (LANES, width)
    return (rows_of(shape) == lanes_of(shape) // head_dim).astype(BF)


def expand(v, spread):
    high = v.astype(BF)
    low = (v - high.astype(F32)).astype(BF)
    return mm(high, spread) + mm(low, spread)


def step_of(dt, ph_ref):
    pre = dt + ph_ref[0:1, :]
    step = jnp.maximum(pre, 0.0) + jnp.log1p(jnp.exp(-jnp.abs(pre)))
    rate = -jnp.exp(ph_ref[1:2, :])
    return pre, step, rate


def lower_mask():
    shape = (CHUNK, CHUNK)
    return rows_of(shape) >= lanes_of(shape)


def pair_rows(v, first):
    return jnp.concatenate([jnp.where(first, v, 0.0), jnp.where(first, 0.0, v)], axis=0)


def as_row(column):
    return jnp.broadcast_to(column, (CHUNK, LANES)).T[0:1, :]


def as_column(row):
    return jnp.broadcast_to(row, (CHUNK, LANES)).T[:, 0:1]


def forward_kernel(px_ref, pbc_ref, ph_ref, gate_ref, x_ref, bcdt_ref, *refs, taps, heads, with_dots):
    if with_dots:
        dmix_ref, gg_ref, y_ref, st_ref, ss_ref, dot_ref = refs
    else:
        gg_ref, y_ref, st_ref, ss_ref = refs
    width = x_ref.shape[1]
    head_dim = width // heads
    states = pbc_ref.shape[1] // 2
    spread = head_map(width, head_dim)
    bcdt = bcdt_ref[...].astype(F32)
    sums = conv(bcdt[:, : 2 * states], pbc_ref, taps)
    bc = sums * jax.nn.sigmoid(sums)
    _, step, rate = step_of(bcdt[:, 2 * states :], ph_ref)
    decay = rate * step
    sums = conv(x_ref[...].astype(F32), px_ref, taps)
    act = sums * jax.nn.sigmoid(sums)
    xs = act * expand(step, spread)
    lower = lower_mask()
    tri = lower.astype(F32)
    first = lanes_of((CHUNK, 2 * head_dim)) < head_dim
    state = None
    chunks = x_ref.shape[0] // CHUNK
    for c in range(chunks):
        span = slice(c * CHUNK, (c + 1) * CHUNK)
        cum = jnp.dot(tri, decay[span], precision=HIGH, preferred_element_type=F32)
        cum_t = cum.T
        b_c = bc[span, :states].astype(BF)
        c_c = bc[span, states:].astype(BF)
        scores = mm_t(c_c, b_c)
        xs_c = xs[span]
        pieces = []
        for p in range(heads // 2):
            two = slice(p * 2 * head_dim, (p + 1) * 2 * head_dim)
            mixes = []
            for h in (2 * p, 2 * p + 1):
                gap = jnp.minimum(cum[:, h : h + 1] - cum_t[h : h + 1, :], 0.0)
                mixes.append(jnp.where(lower, jnp.exp(gap) * scores, 0.0).astype(BF))
            pieces.append(mm(jnp.concatenate(mixes, axis=1), pair_rows(xs_c[:, two], first)))
        y = jnp.concatenate(pieces, axis=1)
        if c > 0:
            y = y + mm(c_c, state) * expand(jnp.exp(cum), spread)
        if c + 1 < chunks:
            last = cum[CHUNK - 1 : CHUNK, :]
            fresh = t_mm(b_c, xs_c * expand(jnp.exp(last - cum), spread))
            state = fresh if c == 0 else fresh + state * expand(jnp.exp(jnp.broadcast_to(last, (states, LANES))), spread)
            st_ref[c] = state
        y = y + px_ref[taps + 1 : taps + 2, :] * act[span]
        y_low = y.astype(BF)
        y_ref[span, :] = y_low
        y = y_low.astype(F32)
        gate = gate_ref[span, :].astype(F32)
        gated = y * (gate * jax.nn.sigmoid(gate))
        ss_ref[c : c + 1, :] = as_row(jnp.sum(gated * gated, axis=1, keepdims=True))
        gg = gated * px_ref[taps + 2 : taps + 3, :]
        gg_ref[span, :] = gg.astype(BF)
        if with_dots:
            dot_ref[c : c + 1, :] = as_row(jnp.sum(gg * dmix_ref[span, :].astype(F32), axis=1, keepdims=True))


def backward_kernel(
    px_ref, pbc_ref, ph_ref, gate_ref, x_ref, bcdt_ref, y_ref, st_ref, dmix_ref, sc_ref,
    dgate_ref, dx_ref, dbcdt_ref, small_ref, *, taps, heads,
):
    length, width = x_ref.shape
    head_dim = width // heads
    states = pbc_ref.shape[1] // 2
    spread = head_map(width, head_dim)

    @pl.when(pl.program_id(0) == 0)
    def _():
        small_ref[...] = jnp.zeros_like(small_ref)

    gx_ref = small_ref.at[:, :width]
    gbc_ref = small_ref.at[:, width : width + 2 * states]
    gh_ref = small_ref.at[:, width + 2 * states :]

    gate = gate_ref[...].astype(F32)
    y = y_ref[...].astype(F32)
    dmix = dmix_ref[...].astype(F32)
    chunks = length // CHUNK
    r = jnp.concatenate([as_column(sc_ref[c : c + 1, :]) for c in range(chunks)], axis=0)
    coef = jnp.concatenate([as_column(sc_ref[chunks + c : chunks + c + 1, :]) for c in range(chunks)], axis=0)
    sig = jax.nn.sigmoid(gate)
    gated = y * gate * sig
    gx_ref[taps + 2 : taps + 3, :] += jnp.sum(dmix * gated * r, axis=0, keepdims=True)
    dgated = r * px_ref[taps + 2 : taps + 3, :] * dmix - coef * gated
    dgate_ref[...] = (dgated * y * (sig * (1.0 + gate * (1.0 - sig)))).astype(BF)
    dy = dgated * gate * sig

    bcdt = bcdt_ref[...].astype(F32)
    bc_in = bcdt[:, : 2 * states]
    bc_sum = conv(bc_in, pbc_ref, taps)
    bc_sig = jax.nn.sigmoid(bc_sum)
    bc = bc_sum * bc_sig
    pre, step, rate = step_of(bcdt[:, 2 * states :], ph_ref)
    decay = rate * step
    x_in = x_ref[...].astype(F32)
    x_sum = conv(x_in, px_ref, taps)
    x_sig = jax.nn.sigmoid(x_sum)
    act = x_sum * x_sig
    step_wide = expand(step, spread)
    xs = act * step_wide
    gx_ref[taps + 1 : taps + 2, :] += jnp.sum(dy * act, axis=0, keepdims=True)

    lower = lower_mask()
    tri = lower.astype(F32)
    upper = (rows_of((CHUNK, CHUNK)) <= lanes_of((CHUNK, CHUNK))).astype(F32)
    last_row = rows_of((CHUNK, LANES)) == CHUNK - 1
    head_lane = lanes_of((CHUNK, LANES))
    head_row = rows_of((LANES, CHUNK))
    first = lanes_of((CHUNK, 2 * head_dim)) < head_dim
    d_state = None
    d_xs, d_bc, d_decay = [None] * chunks, [None] * chunks, [None] * chunks
    for c in reversed(range(chunks)):
        span = slice(c * CHUNK, (c + 1) * CHUNK)
        cum = jnp.dot(tri, decay[span], precision=HIGH, preferred_element_type=F32)
        cum_t = cum.T
        b_c = bc[span, :states].astype(BF)
        c_c = bc[span, states:].astype(BF)
        xs_c = xs[span]
        dy_c = dy[span]
        scores = mm_t(c_c, b_c)
        d_scores = jnp.zeros((CHUNK, CHUNK), F32)
        by_row = jnp.zeros((CHUNK, LANES), F32)
        by_col = jnp.zeros((LANES, CHUNK), F32)
        pieces = []
        for p in range(heads // 2):
            two = slice(p * 2 * head_dim, (p + 1) * 2 * head_dim)
            dy_two = pair_rows(dy_c[:, two], first).astype(BF)
            d_mix = mm_t(dy_two, xs_c[:, two])
            mixes = []
            for i, h in enumerate((2 * p, 2 * p + 1)):
                gap = jnp.minimum(cum[:, h : h + 1] - cum_t[h : h + 1, :], 0.0)
                fall = jnp.where(lower, jnp.exp(gap), 0.0)
                mixes.append((fall * scores).astype(BF))
                d_fall = d_mix[i * CHUNK : (i + 1) * CHUNK] * fall
                d_scores = d_scores + d_fall
                both = d_fall * scores
                by_row = jnp.where(head_lane == h, jnp.sum(both, axis=1, keepdims=True), by_row)
                by_col = jnp.where(head_row == h, jnp.sum(both, axis=0, keepdims=True), by_col)
            pieces.append(t_mm(jnp.concatenate(mixes, axis=0), dy_two))
        d_xs_c = jnp.concatenate(pieces, axis=1)
        d_c = mm(d_scores, b_c)
        d_b = t_mm(d_scores, c_c)
        d_cum = by_row - by_col.T
        new_state = None
        if c > 0:
            before = st_ref[c - 1]
            grow = expand(jnp.exp(cum), spread)
            d_off = dy_c * grow
            new_state = t_mm(c_c, d_off)
            d_c = d_c + mm_t(d_off, before)
            d_cum = d_cum + mm_t(d_off * mm(c_c, before), spread)
        if c + 1 < chunks:
            last = cum[CHUNK - 1 : CHUNK, :]
            tail = expand(jnp.exp(last - cum), spread)
            tailed = xs_c * tail
            d_tailed = mm(b_c, d_state)
            d_b = d_b + mm_t(tailed, d_state)
            d_xs_c = d_xs_c + d_tailed * tail
            lost = mm_t(d_tailed * tailed, spread)
            d_last = jnp.sum(lost, axis=0, keepdims=True)
            if c > 0:
                whole = expand(jnp.exp(jnp.broadcast_to(last, (states, LANES))), spread)
                d_last = d_last + jnp.sum(mm_t(d_state * before * whole, spread), axis=0, keepdims=True)
                new_state = new_state + d_state * whole
            d_cum = d_cum - lost + jnp.where(last_row, d_last, 0.0)
        d_state = new_state
        d_xs[c] = d_xs_c
        d_bc[c] = jnp.concatenate([d_b, d_c], axis=1)
        d_decay[c] = jnp.dot(upper, d_cum, precision=HIGH, preferred_element_type=F32)
    d_xs = jnp.concatenate(d_xs, axis=0)
    d_bc = jnp.concatenate(d_bc, axis=0)
    d_decay = jnp.concatenate(d_decay, axis=0)

    d_step = mm_t(act * d_xs, spread) + d_decay * rate
    gh_ref[1:2, :] += jnp.sum(d_decay * decay, axis=0, keepdims=True)
    d_dt = d_step * jax.nn.sigmoid(pre)
    gh_ref[0:1, :] += jnp.sum(d_dt, axis=0, keepdims=True)

    d_act = dy * px_ref[taps + 1 : taps + 2, :] + d_xs * step_wide
    d_sum = d_act * (x_sig * (1.0 + x_sum * (1.0 - x_sig)))
    d_x, d_taps = conv_back(d_sum, x_in, px_ref, taps)
    dx_ref[...] = d_x.astype(BF)
    for k, value in enumerate(d_taps):
        gx_ref[k : k + 1, :] += value
    d_sum = d_bc * (bc_sig * (1.0 + bc_sum * (1.0 - bc_sig)))
    d_bc_in, d_taps = conv_back(d_sum, bc_in, pbc_ref, taps)
    for k, value in enumerate(d_taps):
        gbc_ref[k : k + 1, :] += value
    dbcdt_ref[:, : 2 * states] = d_bc_in.astype(BF)
    dbcdt_ref[:, 2 * states :] = d_dt.astype(BF)


def per_seq(*dims):
    return pl.BlockSpec((None,) + dims, lambda i: (i,) + (0,) * len(dims))


def fixed(*dims):
    return pl.BlockSpec(dims, lambda i: (0,) * len(dims))


PARAMS = pltpu.CompilerParams(dimension_semantics=("arbitrary",), vmem_limit_bytes=60 << 20)


def run_forward(small, gate, x, bcdt, dmix, taps, heads):
    px, pbc, ph = small
    seqs, length, width = x.shape
    states = pbc.shape[1] // 2
    chunks = length // CHUNK
    more = [] if dmix is None else [dmix]
    sums = [jax.ShapeDtypeStruct((seqs, chunks, LANES), F32)] * (1 + len(more))
    return pl.pallas_call(
        functools.partial(forward_kernel, taps=taps, heads=heads, with_dots=bool(more)),
        grid=(seqs,),
        in_specs=[fixed(*px.shape), fixed(*pbc.shape), fixed(*ph.shape), per_seq(length, width), per_seq(length, width), per_seq(length, bcdt.shape[2])]
        + [per_seq(length, width)] * len(more),
        out_specs=[per_seq(length, width), per_seq(length, width), per_seq(chunks - 1, states, width)] + [per_seq(chunks, LANES)] * len(sums),
        out_shape=[
            jax.ShapeDtypeStruct((seqs, length, width), BF),
            jax.ShapeDtypeStruct((seqs, length, width), BF),
            jax.ShapeDtypeStruct((seqs, chunks - 1, states, width), F32),
        ]
        + sums,
        compiler_params=PARAMS,
        cost_estimate=pl.CostEstimate(flops=seqs * 400_000_000, bytes_accessed=seqs * 4_000_000, transcendentals=seqs * 2_000_000),
        name="mix_forward",
    )(px, pbc, ph, gate, x, bcdt, *more)


def run_backward(small, gate, x, bcdt, y, state, dmix, scalars, taps, heads):
    px, pbc, ph = small
    seqs, length, width = x.shape
    smalls = px.shape[1] + pbc.shape[1] + ph.shape[1]
    return pl.pallas_call(
        functools.partial(backward_kernel, taps=taps, heads=heads),
        grid=(seqs,),
        in_specs=[
            fixed(*px.shape), fixed(*pbc.shape), fixed(*ph.shape), per_seq(length, width), per_seq(length, width),
            per_seq(length, bcdt.shape[2]), per_seq(length, width), per_seq(*state.shape[1:]), per_seq(length, width), per_seq(*scalars.shape[1:]),
        ],
        out_specs=[per_seq(length, width), per_seq(length, width), per_seq(length, bcdt.shape[2]), fixed(8, smalls)],
        out_shape=[
            jax.ShapeDtypeStruct((seqs, length, width), BF),
            jax.ShapeDtypeStruct((seqs, length, width), BF),
            jax.ShapeDtypeStruct((seqs, length, bcdt.shape[2]), BF),
            jax.ShapeDtypeStruct((8, smalls), F32),
        ],
        compiler_params=PARAMS,
        cost_estimate=pl.CostEstimate(flops=seqs * 1_200_000_000, bytes_accessed=seqs * 6_000_000, transcendentals=seqs * 4_000_000),
        name="mix_backward",
    )(px, pbc, ph, gate, x, bcdt, y, state, dmix, scalars)


MESH = pl.DeviceIdType.MESH
VM = pl.BlockSpec(memory_space=pltpu.VMEM)


def partners():
    section = lax.axis_index("section")
    rep = lax.axis_index("rep")
    xb = rep % PAIR
    return section, xb, {"section": 1 - section}, {"rep": rep + 1 - 2 * xb}


def greet(*devices):
    barrier = pltpu.get_barrier_semaphore()
    for device in devices:
        pl.semaphore_signal(barrier, inc=1, device_id=device, device_id_type=MESH)
    pl.semaphore_wait(barrier, len(devices))


def remote(src, dst, send, recv, device):
    return pltpu.make_async_remote_copy(src_ref=src, dst_ref=dst, send_sem=send, recv_sem=recv, device_id=device, device_id_type=MESH)


def sums_kernel(v_ref, out_ref, got_ref, half_ref, send, recv):
    _, _, peer, beside = partners()
    greet(peer, beside)
    first = remote(v_ref, got_ref.at[0], send.at[0], recv.at[0], peer)
    first.start()
    first.wait()
    half_ref[...] = v_ref[...] + got_ref[0]
    second = remote(half_ref, got_ref.at[1], send.at[1], recv.at[1], beside)
    second.start()
    second.wait()
    out_ref[...] = half_ref[...] + got_ref[1]


def run_sums(v, collective_id):
    return pl.pallas_call(
        sums_kernel,
        in_specs=[VM],
        out_specs=VM,
        out_shape=jax.ShapeDtypeStruct(v.shape, F32),
        scratch_shapes=[pltpu.VMEM((2,) + v.shape, F32), pltpu.VMEM(v.shape, F32), pltpu.SemaphoreType.DMA((2,)), pltpu.SemaphoreType.DMA((2,))],
        compiler_params=pltpu.CompilerParams(collective_id=collective_id, has_side_effects=True),
        cost_estimate=pl.CostEstimate(flops=10_000_000, bytes_accessed=20_000_000, transcendentals=0),
        name="token_sums",
    )(v)


def exchange(part_ref, got_a, held, got_x, send, recv, use):
    section, _, peer, beside = partners()
    per = part_ref.shape[1] // CHUNK
    steps = PAIR * per

    def at(i):
        return i // per, pl.ds(pl.multiple_of(i % per * CHUNK, CHUNK), CHUNK)

    def to_peer(i):
        x, span = at(i)
        return remote(part_ref.at[x * 2 + 1 - section, span], got_a.at[i], send.at[0, i], recv.at[0, i], peer)

    def to_beside(i):
        return remote(held.at[i], got_x.at[i], send.at[1, i], recv.at[1, i], beside)

    def start_peer(i, _):
        to_peer(i).start()
        return 0

    def add(i, _):
        to_peer(i).wait_recv()
        x, span = at(i)
        held[i] = (part_ref[x * 2 + section, span].astype(F32) + got_a[i].astype(F32)).astype(BF)

        @pl.when(i > 0)
        def _():
            to_beside(i - 1).start()

        return 0

    def finish(i):
        to_beside(i).wait_recv()
        x, span = at(i)
        use(i, x, span, held[i].astype(F32) + got_x[i].astype(F32))

    def drain(i, _):
        to_peer(i).wait_send()
        to_beside(i).wait_send()
        return 0

    lax.fori_loop(0, steps, start_peer, 0)
    yield
    lax.fori_loop(0, steps, add, 0)
    yield
    to_beside(steps - 1).start()
    yield
    for i in range(steps):
        finish(i)
        yield
    lax.fori_loop(0, steps, drain, 0)


def weights_flow(b, q_ref, o_ref, w_in, w_out, qs, qr, os_, or_, *, ns, ny, split=False):
    section, xb, peer, _ = partners()
    z = lax.axis_index("shard")
    yb = lax.axis_index("rep") // PAIR
    half = ns // 2
    part = q_ref.shape[2] // PARTS
    home = z // half

    def y_peer(k):
        return {"rep": (yb + k) % ny * PAIR + xb}

    def rows_at(h):
        return pl.ds(h * part, part)

    def there(way):
        return z < ns - 1 if way > 0 else z > 0

    def first(src, way, h):
        return remote(src, w_in.at[yb, z, rows_at(h)], qs.at[0, (way + 1) // 2, h], qr.at[yb, z, h], {"shard": z + way})

    def chip(j, h):
        return remote(q_ref.at[1 - b, j, rows_at(h)], w_in.at[j, z, rows_at(h)], qs.at[1, j, h], qr.at[j, z, h], peer)

    def stay(j, h):
        return pltpu.make_async_copy(q_ref.at[b, j, rows_at(h)], w_in.at[j, z, rows_at(h)], qs.at[2 + ny, j, h])

    def onward(place, way, h):
        block = w_in.at[yb, place, rows_at(h)]
        return remote(block, block, qs.at[2, place, h], qr.at[yb, place, h], {"shard": z + way})

    def across(place, k, h):
        block = w_in.at[yb, place, rows_at(h)]
        return remote(block, block, qs.at[2 + k, place, h], qr.at[yb, place, h], y_peer(k))

    def arrival(j, place, h):
        block = w_in.at[j, place, rows_at(h)]
        return remote(block, block, qs.at[2, place, h], qr.at[j, place, h], peer)

    def o_first(src, way):
        return remote(src, w_out.at[z % half, yb], os_.at[0, (way + 1) // 2], or_.at[z % half, yb], {"shard": z + way})

    def o_chip(j):
        return remote(o_ref.at[j], w_out.at[z % half, j], os_.at[1, j], or_.at[z % half, j], peer)

    def o_stay(j):
        return pltpu.make_async_copy(o_ref.at[j], w_out.at[z % half, j], os_.at[1, j])

    def o_onward(k, way):
        block = w_out.at[k, yb]
        return remote(block, block, os_.at[2, k], or_.at[k, yb], {"shard": z + way})

    def o_across(k, i):
        block = w_out.at[k, yb]
        return remote(block, block, os_.at[2 + i, k], or_.at[k, yb], y_peer(i))

    def o_arrival(k, j):
        block = w_out.at[k, j]
        return remote(block, block, os_.at[2, k], or_.at[k, j], peer)

    def along(copy):
        for way in (1, -1):
            @pl.when(there(way))
            def _():
                copy(way).start()

    def start():
        @pl.when(section == b)
        def _():
            for h in range(PARTS):
                chip(yb, h).start()

            @pl.when(home != b)
            def _():
                o_chip(yb).start()

            for h in range(PARTS):
                along(lambda way: first(q_ref.at[b, yb, rows_at(h)], way, h))

            @pl.when(home == b)
            def _():
                along(lambda way: o_first(o_ref.at[yb], way))

            for k in range(ny):
                j = (yb + k) % ny
                for h in range(PARTS):
                    if k:
                        chip(j, h).start()
                    stay(j, h).start()

                @pl.when(home == b)
                def _():
                    o_stay(j).start()

                if k:
                    @pl.when(home != b)
                    def _():
                        o_chip(j).start()

        @pl.when(section != b)
        def _():
            for h in range(PARTS):
                arrival(yb, z, h).wait_recv()
                along(lambda way: first(w_in.at[yb, z, rows_at(h)], way, h))

            @pl.when(home != b)
            def _():
                o_arrival(z % half, yb).wait_recv()
                along(lambda way: o_first(w_out.at[z % half, yb], way))

    def relay_in(d, h=None):
        for h in range(PARTS) if h is None else (h,):
            for way in (1, -1):
                place = z - way * d

                @pl.when((place >= 0) & (place < ns))
                def _():
                    arrival(yb, place, h).wait_recv()

                    @pl.when(there(way))
                    def _():
                        onward(place, way, h).start()

                    for k in range(1, ny):
                        across(place, k, h).start()

    def relay_out(d):
        for way in (1, -1):
            place = z - way * d
            k = place - section * half

            @pl.when((place >= 0) & (place < ns) & (k >= 0) & (k < half))
            def _():
                o_arrival(k, yb).wait_recv()

                @pl.when(there(way))
                def _():
                    o_onward(k, way).start()

                for i in range(1, ny):
                    o_across(k, i).start()

    def finish_in():
        for place in range(ns):
            @pl.when(place != z)
            def _():
                for h in range(PARTS):
                    for k in range(1, ny):
                        arrival((yb + k) % ny, place, h).wait_recv()
                        across(place, k, h).wait_send()

                    @pl.when(jnp.where(place < z, z < ns - 1, z > 0))
                    def _():
                        onward(place, 1, h).wait_send()

        for way in (1, -1):
            @pl.when(there(way))
            def _():
                for h in range(PARTS):
                    first(w_in.at[yb, z, rows_at(h)], way, h).wait_send()

        @pl.when(section != b)
        def _():
            for k in range(1, ny):
                for h in range(PARTS):
                    arrival((yb + k) % ny, z, h).wait_recv()

        @pl.when(section == b)
        def _():
            for j in range(ny):
                for h in range(PARTS):
                    chip(j, h).wait_send()
                    stay(j, h).wait()

    def finish_out():
        @pl.when((section != b) & (home != b))
        def _():
            for k in range(1, ny):
                o_arrival(z % half, (yb + k) % ny).wait_recv()

        @pl.when(section == home)
        def _():
            for way in (1, -1):
                @pl.when(there(way))
                def _():
                    o_first(w_out.at[z % half, yb], way).wait_send()

        for k in range(half):
            place = section * half + k

            @pl.when(place != z)
            def _():
                for i in range(1, ny):
                    o_arrival(k, (yb + i) % ny).wait_recv()
                    o_across(k, i).wait_send()

                @pl.when(jnp.where(place < z, z < ns - 1, z > 0))
                def _():
                    o_onward(k, 1).wait_send()

        @pl.when(section == b)
        def _():
            for j in range(ny):
                @pl.when(home == b)
                def _():
                    o_stay(j).wait()

                @pl.when(home != b)
                def _():
                    o_chip(j).wait_send()

    def relay(d):
        relay_in(d)
        relay_out(d)

    def finish():
        finish_in()
        finish_out()

    if split:
        return start, relay_in, relay_out, finish
    return start, relay, finish


def weights_shapes(q, o, ns):
    ny = q.shape[1]
    outs = [
        jax.ShapeDtypeStruct((ny, ns) + q.shape[2:], BF),
        jax.ShapeDtypeStruct((ns // 2,) + o.shape, BF),
    ]
    dma = pltpu.SemaphoreType.DMA
    sems = [dma((3 + ny, max(ns, 4), PARTS)), dma((ny, ns, PARTS)), dma((2 + ny, max(ns, 2))), dma((ns // 2, ny))]
    return outs, sems


def greet_line(ns, ny):
    section, xb, peer, beside = partners()
    z = lax.axis_index("shard")
    yb = lax.axis_index("rep") // PAIR
    found = [peer, beside] + [{"rep": (yb + k) % ny * PAIR + xb} for k in range(1, ny)]
    for k in (1, ns - 1):
        found += [{"shard": (z + k) % ns}, {"section": 1 - section, "shard": (z + k) % ns}]
    greet(*found)


def start_kernel(tokens_ref, counts_ref, cw_ref, cb_ref, dtb_ref, alg_ref, dsk_ref, pgn_ref, ogn_ref, bc_ref, dt_ref, q_ref, o_ref,
                 all_tokens, normed_ref, live_out_ref, live_ref, px_ref, pbc_ref, ph_ref, gain_ref, wbc_ref, w_in, w_out,
                 small, all_small, mine, packs, full, row8, all_counts,
                 qs, qr, os_, or_, ts, tr, ss, sr, ps, pr, cs, cr, *, ns, ny, taps, heads):
    section, xb, peer, beside = partners()
    z = lax.axis_index("shard")
    yb = lax.axis_index("rep") // PAIR
    half = ns // 2
    greet_all(ns, ny)
    start, relay, finish = weights_flow(0, q_ref, o_ref, w_in, w_out, qs, qr, os_, or_, ns=ns, ny=ny)

    part = cw_ref.shape[1]
    mine[...] = jnp.zeros_like(mine)
    unit3 = LANES
    mine[0:taps, :part] = cw_ref[...].astype(F32)
    mine[taps : taps + 1, :part] = cb_ref[...].astype(F32)
    for i, ref in enumerate((pgn_ref, ogn_ref)):
        mine[taps + 1 + i : taps + 2 + i, : ref.shape[1]] = ref[...].astype(F32)
    for i, ref in enumerate((dtb_ref, alg_ref, dsk_ref)):
        mine[taps + 3 : taps + 4, i * unit3 : i * unit3 + ref.shape[1]] = ref[...].astype(F32)

    def pack_to(k):
        return remote(mine, packs.at[section, z], ps.at[0, k], pr.at[section, z], {"shard": (z + k) % ns})

    def pack_chip(place):
        return remote(packs.at[section, place], packs.at[section, place], ps.at[1, place], pr.at[section, place], peer)

    def pack_from(t, place):
        return remote(mine, packs.at[t, place], ps.at[0, 0], pr.at[t, place], peer)

    counts = remote(counts_ref, all_counts.at[xb], cs, cr, beside)
    counts.start()
    for k in range(1, ns):
        pack_to(k).start()
    remote(mine, packs.at[section, z], ps.at[0, 0], pr.at[section, z], peer).start()
    packs[section, z] = mine[...]
    all_counts[xb] = counts_ref[...]

    def there(way):
        return z < ns - 1 if way > 0 else z > 0

    lanes = bc_ref.shape[1]
    rows = bc_ref.shape[0] // ny
    for j in range(ny):
        small[j] = jnp.zeros_like(small[j])
        small[j, :, :lanes] = bc_ref[j * rows : (j + 1) * rows]
        small[j, :, lanes : lanes + heads] = dt_ref[j * rows : (j + 1) * rows]

    def first(way):
        return remote(small.at[yb], all_small.at[section, z, yb], ss.at[0, (way + 1) // 2, 0], sr.at[section, z, yb], {"shard": z + way})

    def held(place, j):
        return all_small.at[section, place, j]

    def onward(place, way):
        return remote(held(place, yb), held(place, yb), ss.at[1, place, 0], sr.at[section, place, yb], {"shard": z + way})

    def across(place, k):
        return remote(held(place, yb), held(place, yb), ss.at[1 + k, place, 0], sr.at[section, place, yb], {"rep": (yb + k) % ny * PAIR + xb})

    def chip(place, j):
        return remote(held(place, j), held(place, j), ss.at[1 + ny, place, j], sr.at[section, place, j], peer)

    def arrival(b, place, j):
        return remote(all_small.at[b, place, j], all_small.at[b, place, j], ss.at[1, place, 0], sr.at[b, place, j], peer)

    for way in (1, -1):
        @pl.when(there(way))
        def _():
            first(way).start()

    def tokens_beside(m):
        return remote(tokens_ref.at[m], all_tokens.at[section, xb, m], ts.at[0, m], tr.at[section, xb, m], beside)

    def tokens_chip(x, m):
        if x is None:
            return remote(tokens_ref.at[m], all_tokens.at[section, xb, m], ts.at[1, m], tr.at[section, xb, m], peer)
        place = all_tokens.at[section, x, m]
        return remote(place, place, ts.at[2, m], tr.at[section, x, m], peer)

    def tokens_arrival(b, x, m):
        place = all_tokens.at[b, x, m]
        return remote(place, place, ts.at[0, m], tr.at[b, x, m], peer)

    micro, seq_len, _ = tokens_ref.shape
    start()
    for m in range(micro):
        tokens_beside(m).start()
        tokens_chip(None, m).start()
        all_tokens[section, xb, m] = tokens_ref[m]
    for j in range(ny):
        all_small[section, z, j] = small[j]

    def relay_small(d):
        for way in (1, -1):
            place = z - way * d

            @pl.when((place >= 0) & (place < ns))
            def _():
                arrival(section, place, yb).wait_recv()

                @pl.when(there(way))
                def _():
                    onward(place, way).start()

                for k in range(1, ny):
                    across(place, k).start()
                chip(place, yb).start()

    def unpack():
        channels = part * ns
        inner = ogn_ref.shape[1] * ns
        cw = inner // ns // PAIR
        unit = dtb_ref.shape[1] // PAIR
        mine_w = half * cw
        for place in range(ns):
            pack_from(1 - section, place).wait_recv()
        ph_ref[...] = jnp.zeros_like(ph_ref)
        px_ref[...] = jnp.zeros_like(px_ref)
        pbc_ref[...] = jnp.zeros_like(pbc_ref)
        spread = head_map(mine_w, 2 * PAIR * mine_w // heads)
        for b in range(2):
            for at in range(ns):
                full[0 : taps + 1, at * part : (at + 1) * part] = packs[b, at, 0 : taps + 1, :part]
                size = pgn_ref.shape[1]
                gain_ref[b, :, at * size : (at + 1) * size] = packs[b, at, taps + 1 : taps + 2, :size]
            pbc_ref[b, 0 : taps + 1, :] = full[0 : taps + 1, inner:channels]
            row8[...] = jnp.zeros_like(row8)
            for t in range(2):
                for q in range(PAIR):
                    @pl.when((section == t) & (xb == q))
                    def _():
                        for k in range(half):
                            at = t * half + k
                            col = (at * PAIR + q) * cw
                            put = slice(k * cw, (k + 1) * cw)
                            lane = slice(k * unit, (k + 1) * unit)
                            take = slice(q * unit, (q + 1) * unit)
                            px_ref[b, 0 : taps + 1, put] = full[0 : taps + 1, col : col + cw]
                            px_ref[b, taps + 2 : taps + 3, put] = packs[b, at, taps + 2 : taps + 3, q * cw : (q + 1) * cw]
                            ph_ref[b, 0:1, lane] = packs[b, at, taps + 3 : taps + 4, take]
                            ph_ref[b, 1:2, lane] = packs[b, at, taps + 3 : taps + 4, unit3 + q * unit : unit3 + (q + 1) * unit]
                            row8[0:1, lane] = packs[b, at, taps + 3 : taps + 4, 2 * unit3 + q * unit : 2 * unit3 + (q + 1) * unit]
            px_ref[b, taps + 1 : taps + 2, :] = mm(row8[...], spread)[0:1]

    def shared_columns():
        unit = dtb_ref.shape[1] // PAIR
        shape = (wbc_ref.shape[2] - lanes, LANES)
        source, head = rows_of(shape), lanes_of(shape)
        wanted = ((section * half + head // unit) * PAIR + xb) * unit + head % unit
        chosen = ((source == wanted) & (head < half * unit)).astype(BF)
        for b in range(2):
            for at in range(ns):
                for j in range(ny):
                    low = (at * ny + j) * rows
                    wbc_ref[b, low : low + rows, :lanes] = all_small[b, at, j, :, :lanes]
                    wbc_ref[b, low : low + rows, lanes:] = mm(all_small[b, at, j, :, lanes:], chosen).astype(BF)

    def prepare():
        per = seq_len // CHUNK
        for x in range(PAIR):
            for m in range(micro):
                for c in range(per):
                    row = (x * micro + m) * per + c
                    at = lanes_of((1, LANES)).astype(F32) + float(c * CHUNK)
                    live_ref[row : row + 1, :] = (at < all_counts[x, m : m + 1, :]).astype(F32)

        def step(i, _):
            x, m, c = i // (micro * per), i // per % micro, i % per
            span = pl.ds(pl.multiple_of(c * CHUNK, CHUNK), CHUNK)
            wide = all_tokens[0, x, m, span].astype(F32)
            normed_ref[x * micro + m, span] = (wide * rms(wide) * gain_ref[0]).astype(BF)
            live = as_column(live_ref[pl.ds(i, 1), :])
            live_out_ref[x * micro + m, span] = (all_tokens[1, x, m, span].astype(F32) * live).astype(BF)
            return 0

        lax.fori_loop(0, PAIR * micro * per, step, 0)

    relay_small(1)
    for k in range(1, ns):
        pack_from(section, (z + k) % ns).wait_recv()
        pack_chip((z + k) % ns).start()
    for j in range(ny):
        chip(z, j).start()
    for d in range(1, ns):
        if d == ns - 1:
            unpack()
            for m in range(micro):
                tokens_arrival(section, 1 - xb, m).wait_recv()
                tokens_chip(1 - xb, m).start()
            counts.wait_send()
            remote(counts_ref, all_counts.at[1 - xb], cs, cr, beside).wait_recv()
            for m in range(micro):
                for x in range(PAIR):
                    tokens_arrival(1 - section, x, m).wait_recv()
            prepare()
        relay(d)
        if d + 1 < ns:
            relay_small(d + 1)
    for place in range(ns):
        @pl.when(place != z)
        def _():
            for k in range(1, ny):
                j = (yb + k) % ny
                arrival(section, place, j).wait_recv()
                chip(place, j).start()
    for place in range(ns):
        for j in range(ny):
            arrival(1 - section, place, j).wait_recv()
    shared_columns()
    finish()
    for m in range(micro):
        tokens_beside(m).wait_send()
        tokens_chip(None, m).wait_send()
        tokens_chip(1 - xb, m).wait_send()
    for k in range(1, ns):
        pack_to(k).wait_send()
        pack_chip((z + k) % ns).wait_send()
    pack_from(section, z).wait_send()
    for way in (1, -1):
        @pl.when(there(way))
        def _():
            first(way).wait_send()
    for place in range(ns):
        for j in range(ny):
            chip(place, j).wait_send()

        @pl.when(place != z)
        def _():
            for k in range(1, ny):
                across(place, k).wait_send()

            @pl.when(jnp.where(place < z, z < ns - 1, z > 0))
            def _():
                onward(place, 1).wait_send()


def greet_all(ns, ny):
    section, xb, peer, beside = partners()
    z = lax.axis_index("shard")
    yb = lax.axis_index("rep") // PAIR
    found = [peer, beside] + [{"rep": (yb + k) % ny * PAIR + xb} for k in range(1, ny)]
    for k in range(1, ns):
        found += [{"shard": (z + k) % ns}, {"section": 1 - section, "shard": (z + k) % ns}]
    greet(*found)


def run_start(tokens, counts, smalls, bc, dt, q, o, heads):
    conv_weight, _, dt_bias, _, _, _, out_gain = smalls
    ny = q.shape[1]
    ns = heads // dt_bias.shape[1]
    micro, seq_len, width = tokens.shape
    taps = conv_weight.shape[0]
    inner = out_gain.shape[1] * ns
    mine_w = inner // (2 * PAIR)
    states2 = bc.shape[1]
    seqs = PAIR * micro
    outs, sems = weights_shapes(q, o, ns)
    dma = pltpu.SemaphoreType.DMA
    hbm = pl.BlockSpec(memory_space=pl.ANY)
    shape = jax.ShapeDtypeStruct
    rows = bc.shape[0] // ny
    pack = (8, -(-max(conv_weight.shape[1], out_gain.shape[1]) // LANES) * LANES)
    return pl.pallas_call(
        functools.partial(start_kernel, ns=ns, ny=ny, taps=taps, heads=heads),
        in_specs=[VM] * 13,
        out_specs=[VM] * 9 + [hbm, hbm],
        out_shape=[
            shape((2, PAIR) + tokens.shape, BF),
            shape((seqs, seq_len, width), BF),
            shape((seqs, seq_len, width), BF),
            shape((seqs * seq_len // CHUNK, LANES), F32),
            shape((2, 8, mine_w), F32),
            shape((2, 8, states2), F32),
            shape((2, 8, LANES), F32),
            shape((2, 1, width), F32),
            shape((2, width, states2 + LANES), BF),
        ]
        + outs,
        scratch_shapes=[
            pltpu.VMEM((ny, rows, states2 + LANES), BF),
            pltpu.VMEM((2, ns, ny, rows, states2 + LANES), BF),
            pltpu.VMEM(pack, F32),
            pltpu.VMEM((2, ns) + pack, F32),
            pltpu.VMEM((8, conv_weight.shape[1] * ns), F32),
            pltpu.VMEM((8, LANES), F32),
            pltpu.VMEM((PAIR,) + counts.shape, F32),
        ]
        + sems
        + [
            dma((3, 2)), dma((2, PAIR, 2)), dma((2 + ny, max(ns, 2), ny)), dma((2, ns, ny)),
            dma((2, ns)), dma((2, ns)), dma(()), dma(()),
        ],
        compiler_params=comm_params(5),
        cost_estimate=pl.CostEstimate(flops=50_000_000, bytes_accessed=200_000_000, transcendentals=0),
        name="start",
    )(tokens, counts, *smalls, bc, dt, q, o)


def rms(v):
    return lax.rsqrt(jnp.mean(v * v, axis=-1, keepdims=True) + EPSILON)


def spread_out(out_ref, send, recv, peer, per):
    def copy(i, owner):
        span = pl.ds(pl.multiple_of(i % per * CHUNK, CHUNK), CHUNK)
        place = out_ref.at[i // per * 2 + owner, span]
        return remote(place, place, send.at[2, i], recv.at[2, i], peer)

    return copy


def onward_kernel(part_ref, tokens_ref, sums_ref, live_ref, gain_ref, q_ref, o_ref, hidden_ref, normed_ref, rate_ref, gain_out_ref, w_in, w_out,
                  got_a, held, got_x, got_s, half_s, rows_ref, send, recv, send_s, recv_s, rows_s, qs, qr, os_, or_, *, inner, ns, ny):
    section, _, peer, beside = partners()
    per = part_ref.shape[1] // CHUNK
    steps = PAIR * per
    greet_line(ns, ny)
    start, relay_in, relay_out, finish = weights_flow(1, q_ref, o_ref, w_in, w_out, qs, qr, os_, or_, ns=ns, ny=ny, split=True)

    def rows_at(x):
        return pltpu.make_async_copy(tokens_ref.at[0, x, section], rows_ref.at[x], rows_s.at[x])

    for x in range(PAIR):
        rows_at(x).start()
    first = remote(sums_ref, got_s.at[0], send_s.at[0], recv_s.at[0], peer)
    second = remote(half_s, got_s.at[1], send_s.at[1], recv_s.at[1], beside)
    first.start()
    copy = spread_out(hidden_ref, send, recv, peer, per)

    def use(i, x, span, total):
        seq = x * 2 + section
        scale = as_column(rate_ref[pl.ds(seq * per + i % per, 1), :] * live_ref[pl.ds(seq * per + i % per, 1), :])
        gained = scale * total
        gain_out_ref[i] = gained.astype(BF)
        low = (rows_ref[x, span].astype(F32) + gained).astype(BF)
        hidden_ref[seq, span] = low

        @pl.when(i > 0)
        def _():
            copy(i - 1, section).start()

        wide = low.astype(F32)
        normed_ref[seq, span] = (wide * rms(wide) * gain_ref[...]).astype(BF)

    def other(i, _):
        copy(i, section).wait_recv()
        seq = i // per * 2 + 1 - section
        span = pl.ds(pl.multiple_of(i % per * CHUNK, CHUNK), CHUNK)
        wide = hidden_ref[seq, span].astype(F32)
        normed_ref[seq, span] = (wide * rms(wide) * gain_ref[...]).astype(BF)
        return 0

    def drain(i, _):
        copy(i, section).wait_send()
        return 0

    stages = exchange(part_ref, got_a, held, got_x, send, recv, use)
    next(stages)
    first.wait()
    half_s[...] = sums_ref[...] + got_s[0]
    second.start()
    start()
    next(stages)
    next(stages)
    second.wait()
    rate_ref[...] = lax.rsqrt((half_s[...] + got_s[1]) / inner + EPSILON)
    work = [lambda d=d, h=h: relay_in(d, h) if h < PARTS else relay_out(d) for d in range(1, ns) for h in range(PARTS + 1)]

    def relays(count):
        for _ in range(min(count, len(work))):
            work.pop(0)()

    for x in range(PAIR):
        rows_at(x).wait()
    relays(PARTS + 2)
    for _ in range(steps):
        next(stages)
        relays(1)
    copy(steps - 1, section).start()
    lax.fori_loop(0, steps, other, 0)
    for step in work:
        step()
    finish()
    for _ in stages:
        pass
    lax.fori_loop(0, steps, drain, 0)


def back_kernel(part_ref, hidden_ref, tokens_ref, gained_ref, live_ref, gain_ref, out_ref, live_out_ref, dots_ref,
                got_a, held, got_x, dots_own, dots_got, rows_ref, cot_ref, send, recv, send_s, recv_s, rows_s, cot_s):
    section, _, peer, beside = partners()
    per = part_ref.shape[1] // CHUNK
    steps = PAIR * per
    greet(peer, beside)

    def rows_at(x):
        return pltpu.make_async_copy(hidden_ref.at[x * 2 + section], rows_ref.at[x], rows_s.at[x])

    def cot_at(x):
        return pltpu.make_async_copy(tokens_ref.at[1, x, section], cot_ref.at[x], cot_s.at[x])

    for x in range(PAIR):
        rows_at(x).start()
        cot_at(x).start()
    dots_own[...] = jnp.zeros_like(dots_own)
    copy = spread_out(out_ref, send, recv, peer, per)

    def live_of(seq, i):
        return as_column(live_ref[pl.ds(seq * per + i % per, 1), :])

    def use(i, x, span, total):
        seq = x * 2 + section
        rows = rows_ref[x, span].astype(F32)
        inv = rms(rows)
        hat = rows * inv
        d_hat = total * gain_ref[...]
        d_rows = inv * (d_hat - hat * jnp.mean(d_hat * hat, axis=-1, keepdims=True))
        low = (cot_ref[x, span].astype(F32) + d_rows).astype(BF)
        out_ref[seq, span] = low

        @pl.when(i > 0)
        def _():
            copy(i - 1, section).start()

        live = low.astype(F32) * live_of(seq, i)
        live_out_ref[seq, span] = live.astype(BF)
        dots_own[pl.ds(i, 1), :] = as_row(jnp.sum(live * gained_ref[i].astype(F32), axis=1, keepdims=True))

    def other(i, _):
        copy(i, section).wait_recv()
        seq = i // per * 2 + 1 - section
        span = pl.ds(pl.multiple_of(i % per * CHUNK, CHUNK), CHUNK)
        live_out_ref[seq, span] = (out_ref[seq, span].astype(F32) * live_of(seq, i)).astype(BF)
        return 0

    def drain(i, _):
        copy(i, section).wait_send()
        return 0

    stages = exchange(part_ref, got_a, held, got_x, send, recv, use)
    for _ in range(3):
        next(stages)
    for x in range(PAIR):
        rows_at(x).wait()
        cot_at(x).wait()
    for i in range(steps):
        next(stages)
    copy(steps - 1, section).start()
    dots = remote(dots_own, dots_got, send_s.at[0], recv_s.at[0], peer)
    lax.fori_loop(0, steps, other, 0)
    dots.start()
    for _ in stages:
        pass
    lax.fori_loop(0, steps, drain, 0)
    dots.wait()
    for x in range(PAIR):
        for c in range(per):
            i = x * per + c
            dots_ref[pl.ds((x * 2 + section) * per + c, 1), :] = dots_own[i : i + 1, :]
            dots_ref[pl.ds((x * 2 + 1 - section) * per + c, 1), :] = dots_got[i : i + 1, :]


def exchange_scratch(part):
    steps = PAIR * part.shape[1] // CHUNK
    block = (steps, CHUNK, part.shape[2])
    return [pltpu.VMEM(block, BF)] * 3, [pltpu.SemaphoreType.DMA((3, steps)), pltpu.SemaphoreType.DMA((3, steps))]


def own_rows(part):
    return pltpu.VMEM((PAIR,) + part.shape[1:], BF)


def comm_params(collective_id):
    return pltpu.CompilerParams(collective_id=collective_id, has_side_effects=True, vmem_limit_bytes=60 << 20)


def run_onward(part, rows, sums, live, gain, q, o, inner, ns):
    wide, sems = exchange_scratch(part)
    steps = PAIR * part.shape[1] // CHUNK
    small = pltpu.VMEM(sums.shape, F32)
    ny = q.shape[1]
    outs, more = weights_shapes(q, o, ns)
    return pl.pallas_call(
        functools.partial(onward_kernel, inner=inner, ns=ns, ny=ny),
        in_specs=[VM, pl.BlockSpec(memory_space=pl.ANY)] + [VM] * 5,
        out_specs=[VM] * 4 + [pl.BlockSpec(memory_space=pl.ANY)] * 2,
        out_shape=[
            jax.ShapeDtypeStruct(part.shape, BF),
            jax.ShapeDtypeStruct(part.shape, BF),
            jax.ShapeDtypeStruct(sums.shape, F32),
            jax.ShapeDtypeStruct((steps, CHUNK, part.shape[2]), BF),
        ]
        + outs,
        scratch_shapes=wide + [pltpu.VMEM((2,) + sums.shape, F32), small, own_rows(part)] + sems + [pltpu.SemaphoreType.DMA((2,))] * 3 + more,
        compiler_params=comm_params(1),
        cost_estimate=pl.CostEstimate(flops=50_000_000, bytes_accessed=150_000_000, transcendentals=0),
        name="onward",
    )(part, rows, sums, live, gain, q, o)


def run_back(part, hidden, tokens, gained, live, gain):
    wide, sems = exchange_scratch(part)
    small = pltpu.VMEM((8, LANES), F32)
    hbm = pl.BlockSpec(memory_space=pl.ANY)
    return pl.pallas_call(
        back_kernel,
        in_specs=[VM, hbm, hbm, VM, VM, VM],
        out_specs=[VM] * 3,
        out_shape=[
            jax.ShapeDtypeStruct(part.shape, BF),
            jax.ShapeDtypeStruct(part.shape, BF),
            jax.ShapeDtypeStruct(live.shape, F32),
        ],
        scratch_shapes=wide + [small, small, own_rows(part), own_rows(part)] + sems + [pltpu.SemaphoreType.DMA((2,))] * 4,
        compiler_params=comm_params(2),
        cost_estimate=pl.CostEstimate(flops=50_000_000, bytes_accessed=150_000_000, transcendentals=0),
        name="back",
    )(part, hidden, tokens, gained, live, gain)


PARTS = 2
PIECE_ROWS = 48
BLOCK = 16


def by_rows(count, body):
    def step(i, _):
        body(pl.multiple_of(i * BLOCK, BLOCK))
        return 0

    lax.fori_loop(0, count // BLOCK, step, 0)


def line_steps(n):
    return [step for i in range(n - 1) for step in ((1, n - 1 - i), (-1, i))]


def hand_out(b, boards, owns, pc_s, pc_r, *, ny):
    section, xb, peer, beside = partners()
    yb = lax.axis_index("rep") // PAIR

    def y_peer(k):
        return {"rep": (yb + k) % ny * PAIR + xb}

    def y_from(k):
        return (yb + ny - k) % ny

    def span_of(h):
        return pl.ds(pl.multiple_of(h * PIECE_ROWS, PIECE_ROWS), PIECE_ROWS)

    def piece(i, x, y, t, h, kind, device):
        place = boards[i].at[x, y, t, span_of(h)]
        return remote(place, place, pc_s.at[i, kind, x, y, t, h], pc_r.at[i, x, y, t, h], device)

    def offer(i, h):
        return remote(owns[i].at[span_of(h)], boards[i].at[xb, yb, 1 - b, span_of(h)],
                      pc_s.at[i, 0, xb, yb, 1 - b, h], pc_r.at[i, xb, yb, 1 - b, h], peer)

    def gather_chip(i, h):
        @pl.when(section == b)
        def _():
            boards[i][xb, yb, b, span_of(h)] = owns[i][span_of(h)]

        @pl.when(section != b)
        def _():
            offer(i, h).start()

    def gather_side(i, h):
        @pl.when(section == b)
        def _():
            piece(i, xb, yb, 1 - b, h, 0, peer).wait_recv()
            for t in range(2):
                piece(i, xb, yb, t, h, ny, beside).start()

    def gather_y(i, h):
        @pl.when(section == b)
        def _():
            for t in range(2):
                for k in range(1, ny):
                    piece(i, xb, yb, t, h, k, y_peer(k)).start()

    def gather_x(i, h):
        @pl.when(section == b)
        def _():
            for k in range(1, ny):
                for t in range(2):
                    piece(i, xb, y_from(k), t, h, k, peer).wait_recv()
                    piece(i, xb, y_from(k), t, h, ny, beside).start()

    def gather_end(i, h):
        @pl.when(section == b)
        def _():
            for y in range(ny):
                for t in range(2):
                    piece(i, 1 - xb, y, t, h, ny, beside).wait_recv()
                    piece(i, xb, y, t, h, ny, peer).wait_send()
            for t in range(2):
                for k in range(1, ny):
                    piece(i, xb, yb, t, h, k, peer).wait_send()

        @pl.when(section != b)
        def _():
            offer(i, h).wait_send()

    return gather_chip, gather_side, gather_y, gather_x, gather_end


def each(count, body):
    def step(i, _):
        body(i)
        return 0

    lax.fori_loop(0, count, step, 0)


def reduce_flow(b, ga_ref, gb_ref, boards, got_ya, acc_a, got_za, own_a, acc_b, got_zb, own_b, ya_s, ya_r, za_s, za_r, zb_s, zb_r, pc_s, pc_r, *, ns, ny):
    _, xb, peer, _ = partners()
    z = lax.axis_index("shard")
    yb = lax.axis_index("rep") // PAIR
    count = ga_ref.shape[2] // PIECE_ROWS
    steps = line_steps(ns)
    order = []
    for _, target in steps:
        if target not in order:
            order.append(target)
    gather_chip, gather_side, gather_y, gather_x, gather_end = hand_out(b, boards, (own_a, own_b), pc_s, pc_r, ny=ny)

    def y_peer(k):
        return {"rep": (yb + k) % ny * PAIR + xb}

    def span_of(h):
        return pl.ds(pl.multiple_of(h * PIECE_ROWS, PIECE_ROWS), PIECE_ROWS)

    def ya(k, target, h):
        return remote(ga_ref.at[(yb + k) % ny, target, span_of(h)], got_ya.at[k - 1, target, span_of(h)],
                      ya_s.at[k - 1, target, h], ya_r.at[k - 1, target, h], y_peer(k))

    def start(h):
        for target in order:
            @pl.when(target != z)
            def _():
                for k in range(1, ny):
                    ya(k, target, h).start()
        for k in range(1, ny):
            ya(k, z, h).start()

    streams = ((acc_a, got_za, za_s, za_r), (acc_b, got_zb, zb_s, zb_r))

    def line(i, way, target, h):
        acc, got, send, recv = streams[i]
        place = jnp.where(target == z - 1, ns, target) if way < 0 else target
        return remote(acc.at[target, span_of(h)], got.at[place, span_of(h)], send.at[target, h], recv.at[place, h], {"shard": z + way})

    def wait_line(place, h):
        for acc, got, send, recv in streams:
            remote(acc.at[0, span_of(h)], got.at[place, span_of(h)], send.at[0, h], recv.at[place, h], peer).wait_recv()

    def wait_y(target, h):
        for k in range(1, ny):
            remote(ga_ref.at[0, target, span_of(h)], got_ya.at[k - 1, target, span_of(h)], ya_s.at[k - 1, target, h],
                   ya_r.at[k - 1, target, h], peer).wait_recv()

    def add(target, h, into_a, into_b, start, extra):
        span = span_of(h)
        total = ga_ref[yb, target, span].astype(F32)
        for k in range(1, ny):
            total = total + got_ya[k - 1, target, span].astype(F32)
        for place in extra:
            total = total + got_za[place, span].astype(F32)
        into_a[start + (span,)] = total.astype(BF)
        total = gb_ref[target, span].astype(F32)
        for place in extra:
            total = total + got_zb[place, span].astype(F32)
        into_b[start + (span,)] = total.astype(BF)

    def active(way, target):
        return target > z if way > 0 else target < z

    def step(way, target, h):
        wait_y(target, h)
        far = z > 0 if way > 0 else z < ns - 1

        @pl.when(jnp.logical_not(far))
        def _():
            add(target, h, acc_a, acc_b, (target,), ())

        @pl.when(far)
        def _():
            wait_line(target, h)
            add(target, h, acc_a, acc_b, (target,), (target,))

        for i in range(2):
            line(i, way, target, h).start()

    def last(h):
        wait_y(z, h)

        @pl.when(z == 0)
        def _():
            wait_line(ns, h)
            add(z, h, own_a, own_b, (), (ns,))

        @pl.when(z == ns - 1)
        def _():
            wait_line(z, h)
            add(z, h, own_a, own_b, (), (z,))

        @pl.when((z > 0) & (z < ns - 1))
        def _():
            wait_line(z, h)
            wait_line(ns, h)
            add(z, h, own_a, own_b, (), (z, ns))

        for i in range(2):
            gather_chip(i, h)

    def slot(at):
        for way, target in steps:
            h = at - z if way > 0 else at - (ns - 1 - z)

            @pl.when(active(way, target) & (h >= 0) & (h < count))
            def _():
                step(way, target, h)

        mine = at - jnp.where(2 * z > ns - 1, z, ns - 1 - z)
        for late, body in ((0, last), (1, lambda h: [move(i, h) for move in (gather_side, gather_y) for i in range(2)]), (2, lambda h: [gather_x(i, h) for i in range(2)])):
            @pl.when((mine >= late) & (mine < count + late))
            def _():
                body(mine - late)

    def finish():
        def ends(h):
            for i in range(2):
                gather_end(i, h)
            for target in range(ns):
                for k in range(1, ny):
                    ya(k, target, h).wait_send()
            for way, target in steps:
                @pl.when(active(way, target))
                def _():
                    for i in range(2):
                        line(i, way, target, h).wait_send()

        each(count, ends)

    return start, slot, count + ns + 1, finish


def reduce_shapes(ga, gb):
    ny, ns, ra, ca = ga.shape
    rb, cb = gb.shape[1:]
    dma = pltpu.SemaphoreType.DMA
    parts = ra // PIECE_ROWS
    outs = [jax.ShapeDtypeStruct((PAIR, ny, 2, ra, ca), BF), jax.ShapeDtypeStruct((PAIR, ny, 2, rb, cb), BF)]
    scratch = [
        pltpu.VMEM((ny - 1, ns, ra, ca), BF),
        pltpu.VMEM((ns, ra, ca), BF),
        pltpu.VMEM((ns + 1, ra, ca), BF),
        pltpu.VMEM((ra, ca), BF),
        pltpu.VMEM((ns, rb, cb), BF),
        pltpu.VMEM((ns + 1, rb, cb), BF),
        pltpu.VMEM((rb, cb), BF),
        dma((ny - 1, ns, parts)), dma((ny - 1, ns, parts)),
        dma((ns, parts)), dma((ns + 1, parts)),
        dma((ns, parts)), dma((ns + 1, parts)),
        dma((2, ny + 1, PAIR, ny, 2, parts)), dma((2, PAIR, ny, 2, parts)),
    ]
    return outs, scratch


def tail_kernel(ga_ref, gb_ref, pa_ref, pb_ref, vec_ref, p_ref, tokens_ref, cot_all, gain_ref,
                all_a, all_b, vec_out, res_ref, *refs, ns, ny):
    flow, (got_p, held, got_x, give, rows_ref, cot_ref, vec_y, vec_h, vec_z, vec_t, ra_s, ra_r, v_s, v_r, rows_s) = refs[:15], refs[15:]
    section, xb, peer, beside = partners()
    z = lax.axis_index("shard")
    yb = lax.axis_index("rep") // PAIR

    def y_peer(k):
        return {"rep": (yb + k) % ny * PAIR + xb}

    def z_peer(k):
        return {"shard": (z + k) % ns}

    greet(peer, beside, *(y_peer(k) for k in range(1, ny)), *(z_peer(k) for k in range(1, ns)))

    def over_y(k):
        return remote(vec_ref, vec_y.at[k - 1], v_s.at[k], v_r.at[k], y_peer(k))

    def over_z(k):
        return remote(vec_h, vec_z.at[k - 1], v_s.at[ny + k], v_r.at[ny + k], z_peer(k))

    to_chip = remote(vec_t.at[1 - section], vec_out.at[section, xb], v_s.at[0], v_r.at[0], peer)

    def to_side(t):
        return remote(vec_out.at[t, xb], vec_out.at[t, xb], v_s.at[ny + ns + t], v_r.at[ny + ns + t], beside)

    for k in range(1, ny):
        over_y(k).start()

    per = p_ref.shape[1] // CHUNK
    rows_copy = pltpu.make_async_copy(tokens_ref.at[0, xb, section], rows_ref, rows_s.at[0])
    cot_copy = pltpu.make_async_copy(cot_all.at[xb * 2 + section], cot_ref, rows_s.at[1])

    def p_peer(x, c):
        span = pl.ds(c * CHUNK, CHUNK)
        return remote(p_ref.at[x * 2 + 1 - section, span], got_p.at[x, c], ra_s.at[0, x, c], ra_r.at[0, x, c], peer)

    def p_beside(c):
        return remote(held.at[1 - xb, c], got_x.at[c], ra_s.at[1, 0, c], ra_r.at[1, 0, c], beside)

    def p_give(c):
        return remote(give.at[c], res_ref.at[1, pl.ds(c * CHUNK, CHUNK)], ra_s.at[1, 1, c], ra_r.at[1, 1, c], peer)

    boards = (all_a, all_b)
    pieces = flow[13:15]
    chip1, side1, y1, x1, end1 = hand_out(1, boards, (pa_ref, pb_ref), *pieces, ny=ny)
    count = ga_ref.shape[2] // PIECE_ROWS
    start, slot, slots, end0 = reduce_flow(0, ga_ref, gb_ref, boards, *flow, ns=ns, ny=ny)

    def both(body):
        each(count, lambda h: [body(i, h) for i in (1, 0)])

    rows_copy.start()
    cot_copy.start()

    def rows_out():
        for c in range(per):
            for x in range(PAIR):
                p_peer(x, c).start()

    def pieces_side():
        both(side1)

    def pieces_y():
        both(y1)

    def rows_beside():
        for c in range(per):
            for x in range(PAIR):
                p_peer(x, c).wait_recv()

                def body(low):
                    span = pl.ds(low, BLOCK)
                    mine = p_ref[x * 2 + section, pl.ds(c * CHUNK + low, BLOCK)].astype(F32)
                    held[x, c, span] = (mine + got_p[x, c, span].astype(F32)).astype(BF)

                by_rows(CHUNK, body)
            p_beside(c).start()

    def sums_z():
        total = vec_ref[...]
        for k in range(1, ny):
            over_y(k).wait()
            total = total + vec_y[k - 1]
        vec_h[...] = total
        for k in range(1, ns):
            over_z(k).start()

    def pieces_x():
        both(x1)

    def sums_chip():
        total = vec_h[...]
        for k in range(1, ns):
            over_z(k).wait()
            total = total + vec_z[k - 1]
        vec_t[...] = total
        to_chip.start()
        vec_out[section, xb] = vec_t[section]

    def rows_end():
        rows_copy.wait()
        cot_copy.wait()
        for c in range(per):
            p_beside(c).wait_recv()

            def body(low):
                span = pl.ds(low, BLOCK)
                there = pl.ds(c * CHUNK + low, BLOCK)
                total = held[xb, c, span].astype(F32) + got_x[c, span].astype(F32)
                rows = rows_ref[there].astype(F32)
                inv = rms(rows)
                hat = rows * inv
                d_hat = total * gain_ref[...]
                d_rows = inv * (d_hat - hat * jnp.mean(d_hat * hat, axis=-1, keepdims=True))
                low_rows = (cot_ref[there].astype(F32) + d_rows).astype(BF)
                give[c, span] = low_rows

                @pl.when(section == 0)
                def _():
                    res_ref[0, there] = low_rows

            by_rows(CHUNK, body)

        @pl.when(section != 0)
        def _():
            for c in range(per):
                p_give(c).start()

    def sums_side():
        to_chip.wait_send()
        remote(vec_t.at[0], vec_out.at[1 - section, xb], v_s.at[0], v_r.at[0], peer).wait_recv()
        for t in range(2):
            to_side(t).start()

    def sums_end():
        for t in range(2):
            to_side(t).wait_send()
            remote(vec_out.at[t, xb], vec_out.at[t, 1 - xb], v_s.at[ny + ns + t], v_r.at[ny + ns + t], beside).wait_recv()

    ahead = min(3, count)
    rows_out()
    both(chip1)
    each(ahead, start)
    between = ((0, pieces_side), (0, rows_beside), (1, sums_z), (3, sums_chip), (4, rows_end), (5, pieces_y), (6, sums_side), (8, sums_end), (10, pieces_x))

    def go(at, _):
        @pl.when(at + ahead < count)
        def _():
            start(at + ahead)

        slot(at)
        for n, body in between:
            @pl.when(at == n)
            def _():
                body()

        return 0

    lax.fori_loop(0, max(slots, between[-1][0] + 1), go, 0)
    both(end1)
    end0()
    for c in range(per):
        for x in range(PAIR):
            p_peer(x, c).wait_send()
        p_beside(c).wait_send()

        @pl.when(section != 0)
        def _():
            p_give(c).wait_send()

        @pl.when(section == 0)
        def _():
            p_give(c).wait_recv()


def run_tail(ga, gb, pa, pb, vec, p, tokens, cot, gain):
    ny, ns = ga.shape[:2]
    seq_len, width = p.shape[1:]
    per = seq_len // CHUNK
    block = (CHUNK, width)
    dma = pltpu.SemaphoreType.DMA
    hbm = pl.BlockSpec(memory_space=pl.ANY)
    outs, scratch = reduce_shapes(ga, gb)
    return pl.pallas_call(
        functools.partial(tail_kernel, ns=ns, ny=ny),
        in_specs=[VM] * 6 + [hbm, hbm, VM],
        out_specs=[VM] * 4,
        out_shape=outs + [jax.ShapeDtypeStruct((2, PAIR) + vec.shape[1:], F32), jax.ShapeDtypeStruct((2, seq_len, width), BF)],
        scratch_shapes=scratch
        + [
            pltpu.VMEM((PAIR, per) + block, BF),
            pltpu.VMEM((PAIR, per) + block, BF),
            pltpu.VMEM((per,) + block, BF),
            pltpu.VMEM((per,) + block, BF),
            pltpu.VMEM((seq_len, width), BF),
            pltpu.VMEM((seq_len, width), BF),
            pltpu.VMEM((ny - 1,) + vec.shape, F32),
            pltpu.VMEM(vec.shape, F32),
            pltpu.VMEM((ns - 1,) + vec.shape, F32),
            pltpu.VMEM(vec.shape, F32),
            dma((2, PAIR, per)), dma((2, PAIR, per)),
            dma((ny + ns + 2,)), dma((ny + ns + 2,)),
            dma((2,)),
        ],
        compiler_params=comm_params(4),
        cost_estimate=pl.CostEstimate(flops=50_000_000, bytes_accessed=300_000_000, transcendentals=0),
        name="tail",
    )(ga, gb, pa, pb, vec, p, tokens, cot, gain)


def place_kernel(a_ref, b_ref, in_ref, out_ref, dt_ref, *, places, dts, ny):
    for col, size, index, off in places:
        in_ref[:, col : col + size] = a_ref[index + (slice(None), slice(off, off + size))].astype(F32)
    for col, size, index, off in dts:
        dt_ref[:, col : col + size] = a_ref[index + (slice(None), slice(off, off + size))].astype(F32)
    part = b_ref.shape[-1]
    for q in range(PAIR):
        for t in range(2):
            for y in range(ny):
                col = (t * ny + y) * part
                out_ref[q, :, col : col + part] = b_ref[q, y, t].astype(F32)


def run_place(pieces, places, dts, columns, heads, block):
    ny = pieces[0].shape[1]
    rows = pieces[0].shape[3]
    lead = (PAIR, ny, 2)
    width = 2 * ny * pieces[1].shape[4]
    return pl.pallas_call(
        functools.partial(place_kernel, places=places, dts=dts, ny=ny),
        grid=(rows // block,),
        in_specs=[pl.BlockSpec(lead + (block, v.shape[4]), lambda i: (0, 0, 0, i, 0)) for v in pieces],
        out_specs=[
            pl.BlockSpec((block, columns), lambda i: (i, 0)),
            pl.BlockSpec((PAIR, block, width), lambda i: (0, i, 0)),
            pl.BlockSpec((block, heads), lambda i: (i, 0)),
        ],
        out_shape=[
            jax.ShapeDtypeStruct((rows, columns), F32),
            jax.ShapeDtypeStruct((PAIR, rows, width), F32),
            jax.ShapeDtypeStruct((rows, heads), F32),
        ],
        compiler_params=PARAMS,
        cost_estimate=pl.CostEstimate(flops=1_000_000, bytes_accessed=25_000_000, transcendentals=0),
        name="place",
    )(*pieces)


def smalls_kernel(z_ref, v_ref, conv_ref, heads_ref, pre_ref, out_ref, full, *, taps, ns, mine_w, states2, heads, width):
    half = ns // 2
    cw = mine_w // half
    unit = heads // ns // PAIR
    gbc, gh = mine_w, mine_w + states2
    spread = head_map(mine_w, 2 * mine_w * PAIR // heads)
    shared = v_ref[0, 0] + v_ref[0, 1] + v_ref[1, 0] + v_ref[1, 1]
    full[:, 2 * PAIR * mine_w :] = shared[:8, gbc : gbc + states2]
    for t in range(2):
        for q in range(PAIR):
            for k in range(half):
                col = ((t * half + k) * PAIR + q) * cw
                full[:, col : col + cw] = v_ref[t, q, :8, k * cw : (k + 1) * cw]
    channels = (2 * PAIR * mine_w + states2) // ns
    inner = 2 * PAIR * mine_w // ns
    part = width // ns
    wide = v_ref.shape[3]
    skips = []
    for t in range(2):
        skips.append([])
        for q in range(PAIR):
            row = v_ref[t, q, taps + 1 : taps + 2, :mine_w]
            high = row.astype(BF)
            rest = row - high.astype(F32)
            mid = rest.astype(BF)
            rows8 = lambda v: jnp.broadcast_to(v, (8, mine_w))
            skips[t].append((mm_t(rows8(high), spread) + mm_t(rows8(mid), spread) + mm_t(rows8(rest - mid.astype(F32)), spread))[0:1])
    heads_ref[...] = jnp.zeros_like(heads_ref)
    for at in range(ns):
        @pl.when(z_ref[0] == at)
        def _():
            conv_ref[...] = full[:, at * channels : (at + 1) * channels]
            out_ref[...] = full[taps + 2 : taps + 3, at * inner : (at + 1) * inner]
            t, k = at // half, at % half
            for q in range(PAIR):
                span = slice(gh + k * unit, gh + (k + 1) * unit)
                put = slice(q * unit, (q + 1) * unit)
                heads_ref[0:1, put] = v_ref[t, q, 0:1, span]
                heads_ref[1:2, put] = v_ref[t, q, 1:2, span]
                heads_ref[2:3, put] = skips[t][q][:, k * unit : (k + 1) * unit]
            for row in range(-(-width // wide)):
                low, high = max(at * part, row * wide), min((at + 1) * part, (row + 1) * wide)
                if low < high:
                    pre_ref[:, low - at * part : high - at * part] = shared[8 + row : 9 + row, low - row * wide : high - row * wide]


def run_smalls(z, v, taps, ns, mine_w, states2, heads, width):
    channels = (2 * PAIR * mine_w + states2) // ns
    whole = lambda *dims: pl.BlockSpec(dims, lambda i, z: (0,) * len(dims))
    return pl.pallas_call(
        functools.partial(smalls_kernel, taps=taps, ns=ns, mine_w=mine_w, states2=states2, heads=heads, width=width),
        grid_spec=pltpu.PrefetchScalarGridSpec(
            num_scalar_prefetch=1,
            grid=(1,),
            in_specs=[whole(*v.shape)],
            out_specs=[whole(8, channels), whole(8, LANES), whole(1, width // ns), whole(1, 2 * PAIR * mine_w // ns)],
            scratch_shapes=[pltpu.VMEM((8, channels * ns), F32)],
        ),
        out_shape=[
            jax.ShapeDtypeStruct((8, channels), F32),
            jax.ShapeDtypeStruct((8, LANES), F32),
            jax.ShapeDtypeStruct((1, width // ns), F32),
            jax.ShapeDtypeStruct((1, 2 * PAIR * mine_w // ns), F32),
        ],
        compiler_params=PARAMS,
        cost_estimate=pl.CostEstimate(flops=1_000_000, bytes_accessed=1_000_000, transcendentals=0),
        name="smalls",
    )(z, v)


def dot(a, b):
    return jnp.dot(a, b, preferred_element_type=F32)


def pick(index, options):
    result = options[-1]
    for place in reversed(range(len(options) - 1)):
        result = jnp.where(index == place, options[place], result)
    return result


def ordered(index, own, other, axis):
    return jnp.stack([pick(index, (own, other)), pick(index, (other, own))], axis=axis)


def joined(index, own, other, axis):
    return jnp.concatenate([pick(index, (own, other)), pick(index, (other, own))], axis=axis)


def on_device(boundary, lengths, in_proj, dt_proj, out_proj, conv_weight, conv_bias, dt_bias, a_log, d_skip, pre_gain, out_gain):
    ns = lax.axis_size("shard")
    nr = lax.axis_size("rep")
    ny = nr // PAIR
    s = lax.axis_index("section")
    z = lax.axis_index("shard")
    rep = lax.axis_index("rep")
    xb = rep % PAIR
    yb = rep // PAIR

    def swap(v):
        return lax.ppermute(v, "section", [(0, 1), (1, 0)])

    def x_swap(v):
        return lax.ppermute(v, "rep", [(i, i ^ 1) for i in range(nr)])

    def y_send(v, k):
        return lax.ppermute(v, "rep", [(i, (i // PAIR + k) % ny * PAIR + i % PAIR) for i in range(nr)])

    micro, seq_len, width = boundary.shape[1], boundary.shape[3], boundary.shape[4]
    inner = out_proj.shape[1] * ns
    heads = dt_bias.shape[1] * ns
    taps, channels = conv_weight.shape[1], conv_weight.shape[2] * ns
    states2 = channels - inner
    cw = inner // ns // PAIR
    half = ns // 2
    mine_w = half * cw
    mine_h = heads // (2 * PAIR)
    part_w = 2 * mine_w // ny

    def column_chunks(v, first):
        out = []
        for t in range(2):
            for shard in range(t * half, (t + 1) * half):
                start = first + shard * PAIR * cw
                out.append(pick(xb, tuple(v[:, start + q * cw : start + (q + 1) * cw] for q in range(PAIR))))
        return [jnp.concatenate(out[:half], axis=1), jnp.concatenate(out[half:], axis=1)]

    own_in = in_proj[0]
    q_own = []
    for a, b in zip(column_chunks(own_in, 0), column_chunks(own_in, inner)):
        if ny == 2:
            q_own += [a, b]
        else:
            q_own += [v[:, k * part_w : (k + 1) * part_w] for v in (a, b) for k in range(ny // 2)]
    q_own = jnp.stack(q_own).reshape(2, ny, width // ns, part_w)
    own_out = out_proj[0]
    o_own = pick(xb, (own_out[:cw], own_out[cw : 2 * cw])).reshape(ny, cw // ny, width)

    flat = lambda v: v.reshape(-1, v.shape[-1])
    smalls_own = tuple(flat(v) for v in (conv_weight, conv_bias, dt_bias, a_log, d_skip, pre_gain, out_gain))
    counts = jnp.broadcast_to(lengths.astype(F32), (micro, LANES))
    tokens, normed0, g_out1, live8, px, pbc, ph, gains, w_bcdt, in0, out0 = run_start(
        boundary[0, :, 0], counts, smalls_own, own_in[:, 2 * inner :], dt_proj[0], q_own, o_own, heads
    )
    smalls = [(px[b], pbc[b], ph[b]) for b in range(2)]
    unit_h = heads // ns // PAIR
    w_in, w_out = [in0.reshape(ny, width, part_w)], [out0.reshape(mine_w, width)]
    seqs = PAIR * micro

    def by_seq(v):
        return v.reshape((seqs, seq_len) + v.shape[1:])

    def of_own(v):
        return pick(xb, (v[0], v[1]))

    chunks = seq_len // CHUNK

    def forward(b, normed, dmix):
        normed = normed.reshape(seqs * seq_len, width)
        proj = [dot(normed, w_in[b][j]).astype(BF) for j in range(ny)]
        if ny > 2:
            proj = [jnp.concatenate(proj[: ny // 2], axis=1), jnp.concatenate(proj[ny // 2 :], axis=1)]
        gate, x = by_seq(proj[0]), by_seq(proj[1])
        bcdt = by_seq(dot(normed, w_bcdt[b]))
        gg, y, state, *sums = run_forward(smalls[b], gate, x, bcdt, dmix, taps, mine_h)
        gg = gg.reshape(seqs * seq_len, mine_w)
        part = by_seq(dot(gg, w_out[b]).astype(BF))
        return part, sums, (normed, gate, x, bcdt, gg, y, state)

    def mixed_back(b, g_out):
        dmix = lax.dot_general(g_out, w_out[b], (((1,), (1,)), ((), ())), preferred_element_type=F32)
        return by_seq(dmix.astype(BF))

    part0, sums, stored0 = forward(0, normed0, None)
    hidden, normed, r0, gained0, in1, out1 = run_onward(
        part0, tokens, sums[0].reshape(seqs * chunks, LANES), live8, gains[1], q_own, o_own, float(inner), ns
    )
    w_in.append(in1.reshape(ny, width, part_w))
    w_out.append(out1.reshape(mine_w, width))
    g_out1 = g_out1.reshape(seqs * seq_len, width)
    dmix1 = mixed_back(1, g_out1)
    part1, sums, stored1 = forward(1, normed, dmix1)
    both_sums = run_sums(jnp.concatenate([v.reshape(seqs * chunks, LANES) for v in sums]), 3)
    r1 = lax.rsqrt(both_sums[: seqs * chunks] / inner + EPSILON)

    def backward(b, dmix, stored, r, coef):
        normed, gate, x, bcdt, _, y, state = stored
        scalars = jnp.concatenate([r.reshape(seqs, chunks, LANES), coef.reshape(seqs, chunks, LANES)], axis=1)
        dgate, dx, dbcdt, gsmall = run_backward(smalls[b], gate, x, bcdt, y, state, dmix, scalars, taps, mine_h)
        flat = lambda v: v.reshape(seqs * seq_len, v.shape[-1])
        dgate, dx, dbcdt = flat(dgate), flat(dx), flat(dbcdt)
        if ny == 2:
            dparts = [dgate, dx]
        else:
            dparts = [v[:, k * part_w : (k + 1) * part_w] for v in (dgate, dx) for k in range(ny // 2)]
        against = lambda a, w: lax.dot_general(a, w, (((1,), (1,)), ((), ())), preferred_element_type=F32)
        d_normed = against(dbcdt, w_bcdt[b])
        for j in range(ny):
            d_normed = d_normed + against(dparts[j], w_in[b][j])
        gpre = jnp.sum(d_normed * normed.astype(F32), axis=0) / gains[b, 0]
        across = lambda a, c: lax.dot_general(a, c, (((0,), (0,)), ((), ())), preferred_element_type=F32)

        dbc = dbcdt[:, :states2]
        cols = [dbc[:, : states2 // 2], dbc[:, states2 // 2 :]]
        total = (pick(s, cols).astype(F32) + swap(pick(s, cols[::-1])).astype(F32)).astype(BF)
        cols = [total[:, : states2 // 4], total[:, states2 // 4 :]]
        total = (pick(xb, cols).astype(F32) + x_swap(pick(xb, cols[::-1])).astype(F32)).astype(BF)
        mine = jnp.concatenate([total, dbcdt[:, states2 : states2 + states2 // 4]], axis=1)
        grad_in = [across(normed, jnp.concatenate([v, mine], axis=1)).astype(BF) for v in dparts]
        grad_in = [v.reshape(ns, width // ns, -1) for v in grad_in]
        wide = gsmall.shape[1]
        gpre = jnp.pad(gpre, (0, 8 * wide - width)).reshape(8, wide)
        return by_seq(d_normed.astype(BF)), grad_in, jnp.concatenate([gsmall, gpre])

    def z_sum(v):
        parts = [v[j] for j in range(ns)]
        total = pick(z, parts).astype(F32)
        for k in range(1, ns):
            send = lax.dynamic_index_in_dim(v, (z + k) % ns, 0, False)
            got = lax.ppermute(send, "shard", [(i, (i + k) % ns) for i in range(ns)])
            total = total + got.astype(F32)
        return total.astype(BF)

    def out_chip(g_out, gg, r):
        g_scaled = (g_out.astype(F32) * r.reshape(-1, 1)).astype(BF)
        across = lambda a, c: lax.dot_general(a, c, (((0,), (0,)), ((), ())), preferred_element_type=F32)
        grad = across(gg, g_scaled).astype(BF)
        cols = [grad[:, : width // 2], grad[:, width // 2 :]]
        send = pick(s, cols[::-1])
        got = swap(send)
        return joined(s, pick(s, cols), got, 0)

    def out_grad(v):
        step = width // 2 // ny
        parts = [v[:, j * step : (j + 1) * step] for j in range(ny)]
        total = pick(yb, parts).astype(F32)
        for k in range(1, ny):
            send = pick((yb + k) % ny, parts)
            got = y_send(send, k)
            total = total + got.astype(F32)
        return total.astype(BF).reshape(ns, cw, -1)

    v1 = out_chip(g_out1, stored1[4], r1)
    gout1 = out_grad(v1)
    d_normed1, gin1, gsmall1 = backward(1, dmix1, stored1, r1, r1 * r1 * r1 * both_sums[seqs * chunks :] / inner)
    piece_b1 = z_sum(gout1)
    d_normed1, *gin1 = lax.optimization_barrier((d_normed1, *gin1))
    total1 = pick(yb, gin1).astype(F32)
    for k in range(1, ny):
        send = pick((yb + k) % ny, gin1)
        got = y_send(send, k)
        total1 = total1 + got.astype(F32)
    total1 = total1.astype(BF)
    cot0, g_out0, dots0 = run_back(d_normed1, hidden, tokens, gained0, live8, gains[1])

    g_out0 = g_out0.reshape(-1, width)
    dmix0 = mixed_back(0, g_out0)
    v0 = out_chip(g_out0, stored0[4], r0)
    dmix0, total1 = lax.optimization_barrier((dmix0, total1))
    gout0 = out_grad(v0)
    piece_a1 = z_sum(total1)

    part1 = part1.reshape(PAIR, micro, seq_len, width)
    mine = pick(s, (part1[:, 0], part1[:, 1])).astype(F32) + swap(pick(s, (part1[:, 1], part1[:, 0]))).astype(F32)
    mine = mine.astype(BF)
    send = of_own(mine[::-1])
    got = x_swap(send)
    mine = of_own(mine).astype(F32) + got.astype(F32)
    own_hidden = of_own(hidden.reshape(PAIR, micro, seq_len, width))
    scale = of_own((live8 * r1).reshape(PAIR, micro, seq_len, 1))
    final = (pick(s, (own_hidden[0], own_hidden[1])).astype(F32) + pick(s, (scale[0], scale[1])) * mine).astype(BF)
    final = ordered(s, final, swap(final), 0)

    d_normed0, gin0, gsmall0 = backward(0, dmix0, stored0, r0, r0 * r0 * dots0 / inner)
    *pieces, vec, res = run_tail(
        jnp.stack(gin0), gout0, piece_a1, piece_b1, jnp.stack([gsmall0, gsmall1]), d_normed0, tokens, cot0, gains[0]
    )
    activations = pick(s, (own_hidden, final))
    input_grads = pick(s, (res, of_own(cot0.reshape(PAIR, micro, seq_len, width))))
    places, dts = [], []
    col = 0
    for plane in range(2):
        for t in range(2):
            for k in range(half):
                for q in range(PAIR):
                    y_at, off = divmod(plane * mine_w + k * cw, part_w)
                    places.append((col, cw, (q, y_at, t), off))
                    col += cw
    quad = states2 // 4
    for t in range(2):
        for q in range(PAIR):
            places.append((col, quad, (q, 0, t), part_w))
            col += quad
    for t in range(2):
        for k in range(half):
            for q in range(PAIR):
                dts.append((((t * half + k) * PAIR + q) * unit_h, unit_h, (q, 0, t), part_w + quad + k * unit_h))
    grad_in, grad_out, grad_dt = run_place(pieces, tuple(places), tuple(dts), col, heads, 64)
    grad_out = grad_out.reshape(PAIR * cw, width)
    g_conv, g_heads, g_pre, g_og = run_smalls(z[None], vec, taps, ns, mine_w, states2, heads, width)
    g_cw, g_cb = g_conv[:taps], g_conv[taps]
    g_dtb, g_alg, g_dsk = (g_heads[i, : heads // ns] for i in range(3))
    g_pre, g_og = g_pre[0], g_og[0]

    return (
        activations[None, :, None],
        input_grads[None, :, None],
        grad_in[None],
        grad_dt[None],
        grad_out[None],
        g_cw[None],
        g_cb[None],
        g_dtb[None],
        g_alg[None],
        g_dsk[None],
        g_pre[None],
        g_og[None],
    )


def solution(mesh):
    shard1 = P("section", "shard")
    shard2 = P("section", "shard", None)
    tokens = P("section", None, ("shard", "rep"), None, None)
    taps = P("section", None, "shard")
    weights = (shard2, shard2, shard2, taps, shard1, shard1, shard1, shard1, shard1, shard1)
    return jax.shard_map(
        on_device,
        mesh=mesh,
        in_specs=(tokens, P(None, ("shard", "rep"))) + weights,
        out_specs=(tokens, tokens) + weights,
        check_vma=False,
    )
```

profile of v0, /device:TPU:0, one launch (start us, length us, event | category | flops | bytes accessed | tf_op | source)
XLA Modules:
  0.0 720.0 jit_solution(12416352704239546061)
XLA Ops:
  4.5 2.8 slice_select_fusion.11
  11.3 87.8 %start.1 = (bf16[2,2,2,256,1536]{4,3,2,1,0:T(8,128)(2,1)}, bf16[4,256,1536]{2,1,0:T(8,128)(2,1)}, bf16[4,256,1536]{2,1,0:T(8,128)(2,1)}, f32[8,128]{1,0:T(8,128)...) custom-call(bf16[2,256,1536]{2,1,0:T(8,128)(2,1)} %bitcast.238, ...), custom_call_target="tpu_custom_call" | custom-call | flops 50000000 | bytes 200000000 | tf_op jit(solution)/shard_map/start/pallas_call | solution.py:963
  103.1 2.8 fusion.38
  106.4 3.7 convolution_convert_fusion.11
  110.1 3.7 convolution_convert_fusion.10
  113.7 3.0 fusion.19.bcdt_ref
  117.3 11.9 %mix_forward.2 = (bf16[4,256,768]{2,1,0:T(8,128)(2,1)}, bf16[4,256,768]{2,1,0:T(8,128)(2,1)}, f32[4,1,128,768]{3,2,1,0:T(8,128)}, f32[4,2,128]{2,1,0:T(2,128)}) custom-call(f32[8,768]{1,0:T(8,128)} %get-tuple-element.173.px_ref, f32[8,256]{1,0:T(8,128)} %get-tuple-element.175.pbc_ref, f32[8,128]{1,0:T(8,128)} %get-tuple-element.182.ph_ref, ...), custom_call_target="tpu_custom_call" | custom-call | flops 1600000000 | bytes 16000000 | tf_op jit(solution)/shard_map/mix_forward/pallas_call | solution.py:314
  129.2 6.4 convolution_convert_fusion.1
  135.6 79.5 %onward.1 = (bf16[4,256,1536]{2,1,0:T(8,128)(2,1)}, bf16[4,256,1536]{2,1,0:T(8,128)(2,1)}, f32[8,128]{1,0:T(8,128)}, bf16[4,128,1536]{2,1,0:T(8,128)(2,1)}, bf16...) custom-call(bf16[4,256,1536]{2,1,0:T(8,128)(2,1)} %bitcast.227, ...), custom_call_target="tpu_custom_call" | custom-call | flops 50000000 | bytes 150000000 | tf_op jit(solution)/shard_map/onward/pallas_call | solution.py:1183
  215.2 2.8 fusion.37
  218.5 3.0 fusion.16.bcdt_ref
  221.4 3.7 convolution_convert_fusion.9
  225.1 3.7 convolution_convert_fusion.8
  228.8 3.8 convolution_convert_fusion.7
  232.6 12.4 %mix_forward.3 = (bf16[4,256,768]{2,1,0:T(8,128)(2,1)}, bf16[4,256,768]{2,1,0:T(8,128)(2,1)}, f32[4,1,128,768]{3,2,1,0:T(8,128)}, f32[4,2,128]{2,1,0:T(2,128)}, f32[4,2,128]{2,1,0:T(2,128)}) custom-call(f32[8,768]{1,0:T(8,128)} %get-tuple-element.172.px_ref, f32[8,256]{1,0:T(8,128)} %get-tuple-element.174.pbc_ref, f32[8,128]{1,0:T(8,128)} %get-tuple-element.181.ph_ref, ...), custom_call_target="tpu_custom_call" | custom-call | flops 1600000000 | bytes 16000000 | tf_op jit(solution)/shard_map/mix_forward/pallas_call | solution.py:314
  245.0 4.7 convolution_convert_fusion
  251.9 6.4 collective-permute-start
  258.9 6.5 token_sums.1
  266.7 23.8 %mix_backward.2 = (bf16[4,256,768]{2,1,0:T(8,128)(2,1)}, bf16[4,256,768]{2,1,0:T(8,128)(2,1)}, bf16[4,256,384]{2,1,0:T(8,128)(2,1)}, f32[8,1152]{1,0:T(8,128)}) custom-call(f32[8,768]{1,0:T(8,128)} %get-tuple-element.172.px_ref, f32[8,256]{1,0:T(8,128)} %get-tuple-element.174.pbc_ref, f32[8,128]{1,0:T(8,128)} %get-tuple-element.181.ph_ref, ...), custom_call_target="tpu_custom_call" | custom-call | flops 4800000000 | bytes 24000000 | tf_op jit(solution)/shard_map/mix_backward/pallas_call | solution.py:336
  292.3 5.2 bitcast_convert_fusion
  303.3 2.6 fusion.41
  306.0 2.6 fusion.40
  308.7 3.7 multiply_reduce_fusion
  314.4 7.9 %collective-permute-done.4 = bf16[1024,64]{1,0:T(8,128)(2,1)S(1)} collective-permute-done((bf16[1024,64]{1,0:T(8,128)(2,1)S(1)}, bf16[1024,64]{1,0:T(8,128)(2,1)S(1)}, u32[]{:S(2)}, u32[]{:S(2)}) %collective-permute-start.4) | collective-permute-done | bytes 131104 | tf_op jit(solution)/shard_map/ppermute | solution.py:1823
  322.5 6.2 convolution_convert_fusion.5
  328.7 3.9 convolution_convert_fusion.4
  335.7 47.3 %back.1 = (bf16[4,256,1536]{2,1,0:T(8,128)(2,1)}, bf16[4,256,1536]{2,1,0:T(8,128)(2,1)}, f32[8,128]{1,0:T(8,128)}) custom-call(bf16[4,256,1536]{2,1,0:T(8,128)(2,1)} %bitcast.197, bf16[4,256,1536]{2,1,0:T(8,128)(2,1)} %get-tuple-element.77.hidden_ref, bf16[2,2,2,256,1536]{4,3,2,1,0:T(8,128)(2,1)} %get-tuple-element.73.tokens_ref, ...), custom_call_target="tpu_custom_call" | custom-call | flops 50000000 | bytes 150000000 | tf_op jit(solution)/shard_map/back/pallas_call | solution.py:1205
  383.0 5.3 bitcast_convert_fusion.1
  390.2 3.7 convolution_convert_fusion.6
  402.0 22.7 %collective-permute-done.14 = bf16[1536,384]{1,0:T(8,128)(2,1)S(1)} collective-permute-done((bf16[1536,384]{1,0:T(8,128)(2,1)S(1)}, bf16[1536,384]{1,0:T(8,128)(2,1)S(1)}, u32[]{:S(2)}, u32[]{:S(2)}) %collective-permute-start.14) | collective-permute-done | bytes 1179680 | tf_op jit(solution)/shard_map/ppermute | solution.py:1826
  425.3 3.3 collective-permute-start.17
  430.9 6.3 collective-permute-done.17
  437.2 12.5 %collective-permute-done.16 = bf16[384,384]{1,0:T(8,128)(2,1)S(1)} collective-permute-done((bf16[384,384]{1,0:T(8,128)(2,1)S(1)}, bf16[384,384]{1,0:T(8,128)(2,1)S(1)}, u32[]{:S(2)}, u32[]{:S(2)}) %collective-permute-start.16) | collective-permute-done | bytes 294944 | tf_op jit(solution)/shard_map/ppermute | solution.py:1939
  453.1 2.9 add_convert_fusion
  456.0 23.4 %mix_backward.3 = (bf16[4,256,768]{2,1,0:T(8,128)(2,1)}, bf16[4,256,768]{2,1,0:T(8,128)(2,1)}, bf16[4,256,384]{2,1,0:T(8,128)(2,1)}, f32[8,1152]{1,0:T(8,128)}) custom-call(f32[8,768]{1,0:T(8,128)} %get-tuple-element.173.px_ref, f32[8,256]{1,0:T(8,128)} %get-tuple-element.175.pbc_ref, f32[8,128]{1,0:T(8,128)} %get-tuple-element.182.ph_ref, ...), custom_call_target="tpu_custom_call" | custom-call | flops 4800000000 | bytes 24000000 | tf_op jit(solution)/shard_map/mix_backward/pallas_call | solution.py:336
  483.8 4.7 collective-permute-start.11
  490.5 2.6 fusion.43
  493.2 2.6 fusion.42
  496.1 3.7 fusion.36
  511.1 5.3 collective-permute-done.7
  516.6 5.8 convolution_convert_fusion.2
  522.4 3.9 convolution_convert_fusion.3
  526.3 3.0 pad_maximum_fusion.ga_ref
  529.3 19.8 %collective-permute-done.11 = bf16[384,896]{1,0:T(8,128)(2,1)} collective-permute-done((bf16[384,896]{1,0:T(8,128)(2,1)}, bf16[384,896]{1,0:T(8,128)(2,1)}, u32[]{:S(2)}, u32[]{:S(2)}) %collective-permute-start.11) | collective-permute-done | bytes 688160 | tf_op jit(solution)/shard_map/ppermute | solution.py:1939
  549.2 3.0 fusion.13.pa_ref
  552.1 147.6 %tail.1 = (bf16[2,2,2,384,896]{4,3,2,1,0:T(8,128)(2,1)}, bf16[2,2,2,384,384]{4,3,2,1,0:T(8,128)(2,1)}, f32[2,2,16,1152]{3,2,1,0:T(8,128)}, bf16[2,256,1536]{2,1,0:T(8,128)(2,1)}) custom-call(bf16[2,4,384,896]{3,2,1,0:T(8,128)(2,1)} %pad_maximum_fusion.ga_ref, bf16[4,384,384]{2,1,0:T(8,128)(2,1)} %bitcast.218, bf16[384,896]{1,0:T(8,128)(2,1)} %fusion.13.pa_ref, ...), custom_call_target="tpu_custom_call" | custom-call | flops 50000000 | bytes 300000000 | tf_op jit(solution)/shard_map/tail/pallas_call | solution.py:1655
  704.5 2.8 select_bitcast_fusion
  707.2 9.3 %place.1 = (f32[384,6400]{1,0:T(8,128)}, f32[2,384,1536]{2,1,0:T(8,128)}, f32[384,48]{1,0:T(8,128)}) custom-call(bf16[2,2,2,384,896]{4,3,2,1,0:T(8,128)(2,1)} %get-tuple-element.108.a_ref, bf16[2,2,2,384,384]{4,3,2,1,0:T(8,128)(2,1)} %get-tuple-element.109.b_ref), custom_call_target="tpu_custom_call" | custom-call | flops 1000000 | bytes 25000000 | tf_op jit(solution)/shard_map/place/pallas_call | solution.py:1700
  (189 shorter events, 72.1 us)
Async XLA Ops:
  4.4 3.1 copy-start.22
  103.1 3.3 copy-start.14
  105.9 4.1 copy-start.23
  105.9 4.1 copy-start.25
  110.1 3.7 copy-start.20
  113.7 3.0 copy-start.35
  215.1 3.3 copy-start.17
  218.0 3.5 copy-start.27
  218.0 7.1 copy-start.29
  225.1 3.7 copy-start.39
  225.1 3.7 copy-start.42
  249.7 8.6 %copy-start.37 = (f32[4,2,128]{2,1,0:T(2,128)S(1)}, f32[4,2,128]{2,1,0:T(2,128)}, u32[]{:S(2)}) copy-start(f32[4,2,128]{2,1,0:T(2,128)} %get-tuple-element.82) | copy-start | bytes 12292
  249.7 8.5 %copy-start.38 = (f32[4,2,128]{2,1,0:T(2,128)S(1)}, f32[4,2,128]{2,1,0:T(2,128)}, u32[]{:S(2)}) copy-start(f32[4,2,128]{2,1,0:T(2,128)} %get-tuple-element.83) | copy-start | bytes 12292
  249.7 15.7 %copy-start.32 = (f32[8,128]{1,0:T(8,128)S(1)}, f32[8,128]{1,0:T(8,128)}, u32[]{:S(2)}) copy-start(f32[8,128]{1,0:T(8,128)} %get-tuple-element.75.live_ref) | copy-start | bytes 12292
  251.9 144.5 %collective-permute-start = (bf16[2,256,1536]{2,1,0:T(8,128)(2,1)}, bf16[2,256,1536]{2,1,0:T(8,128)(2,1)}, u32[]{:S(2)}, u32[]{:S(2)}) collective-permute-start(bf16[2,256,1536]{2,1,0:T(8,128)(2,1)} %select_bitcast_fusion.1), channel_id=1, source_target_pairs={{0,16},{16,0},{1,17},{17,1},{2,18},{18,2},{3,19},{19,3},{4,20},{20... | collective-permute-start | bytes 4718600 | tf_op jit(solution)/shard_map/ppermute | solution.py:1820
  292.3 21.0 %collective-permute-start.3 = (bf16[1024,128]{1,0:T(8,128)(2,1)}, bf16[1024,128]{1,0:T(8,128)(2,1)S(1)}, u32[]{:S(2)}, u32[]{:S(2)}) collective-permute-start(bf16[1024,128]{1,0:T(8,128)(2,1)} %broadcast_select_fusion.12), channel_id=1, source_target_pairs={{0,16},{16,0},{1,17},{17,1},{2,18},{18,2},{3,19},{19,3},{4,20},{20... | collective-permute-start | bytes 786440 | tf_op jit(solution)/shard_map/ppermute | solution.py:1820
  297.5 4.5 copy-start.9
  297.5 3.2 copy-start
  298.6 95.3 %collective-permute-start.13 = (bf16[768,768]{1,0:T(8,128)(2,1)}, bf16[768,768]{1,0:T(8,128)(2,1)}, u32[]{:S(2)}, u32[]{:S(2)}) collective-permute-start(bf16[768,768]{1,0:T(8,128)(2,1)} %broadcast_select_fusion.5), channel_id=1, source_target_pairs={{0,16},{16,0},{1,17},{17,1},{2,18},{18,2},{3,19},{19,3},{4,20},{20... | collective-permute-start | bytes 3538952 | tf_op jit(solution)/shard_map/ppermute | solution.py:1820
  308.7 3.8 copy-start.33
  308.7 3.9 copy-start.34
  313.5 8.8 %collective-permute-start.4 = (bf16[1024,64]{1,0:T(8,128)(2,1)S(1)}, bf16[1024,64]{1,0:T(8,128)(2,1)S(1)}, u32[]{:S(2)}, u32[]{:S(2)}) collective-permute-start(bf16[1024,64]{1,0:T(8,128)(2,1)S(1)} %broadcast_select_fusion.14), channel_id=1, source_target_pairs={{0,1},{1,0},{2,3},{3,2},{4,5},{5,4},{6,7},{7,6},{8,9},{9,8},{10,11... | collective-permute-start | bytes 393224 | tf_op jit(solution)/shard_map/ppermute | solution.py:1823
  322.5 6.2 copy-start.19
  322.5 6.2 copy-start.44
  328.7 3.9 copy-start.5
  334.2 118.0 %collective-permute-start.5 = (bf16[4,384,896]{2,1,0:T(8,128)(2,1)S(1)}, bf16[4,384,896]{2,1,0:T(8,128)(2,1)}, u32[]{:S(2)}, u32[]{:S(2)}) collective-permute-start(bf16[4,384,896]{2,1,0:T(8,128)(2,1)S(1)} %broadcast_select_fusion), channel_id=1, source_target_pairs={{0,2},{1,3},{2,0},{3,1},{4,6},{5,7},{6,4},{7,5},{8,10},{9,11},{10,... | collective-permute-start | bytes 8257544 | tf_op jit(solution)/shard_map/ppermute | solution.py:1826
  383.0 6.6 copy-start.41
  388.5 12.4 %collective-permute-start.8 = (bf16[768,768]{1,0:T(8,128)(2,1)S(1)}, bf16[768,768]{1,0:T(8,128)(2,1)S(1)}, u32[]{:S(2)}, u32[]{:S(2)}) collective-permute-start(bf16[768,768]{1,0:T(8,128)(2,1)S(1)} %broadcast_select_fusion.9), channel_id=1, source_target_pairs={{0,16},{16,0},{1,17},{17,1},{2,18},{18,2},{3,19},{19,3},{4,20},{20... | collective-permute-start | bytes 3538952 | tf_op jit(solution)/shard_map/ppermute | solution.py:1820
  390.2 3.7 copy-start.10
  395.8 28.9 %collective-permute-start.14 = (bf16[1536,384]{1,0:T(8,128)(2,1)S(1)}, bf16[1536,384]{1,0:T(8,128)(2,1)S(1)}, u32[]{:S(2)}, u32[]{:S(2)}) collective-permute-start(bf16[1536,384]{1,0:T(8,128)(2,1)S(1)} %broadcast_select_fusion.1), channel_id=1, source_target_pairs={{0,2},{1,3},{2,0},{3,1},{4,6},{5,7},{6,4},{7,5},{8,10},{9,11},{10,... | collective-permute-start | bytes 3538952 | tf_op jit(solution)/shard_map/ppermute | solution.py:1826
  399.5 29.1 %collective-permute-start.1 = (bf16[256,1536]{1,0:T(8,128)(2,1)S(1)}, bf16[256,1536]{1,0:T(8,128)(2,1)S(1)}, u32[]{:S(2)}, u32[]{:S(2)}) collective-permute-start(bf16[256,1536]{1,0:T(8,128)(2,1)S(1)} %select_bitcast_fusion.4), channel_id=1, source_target_pairs={{0,1},{1,0},{2,3},{3,2},{4,5},{5,4},{6,7},{7,6},{8,9},{9,8},{10,11... | collective-permute-start | bytes 2359304 | tf_op jit(solution)/shard_map/ppermute | solution.py:1823
  401.4 28.0 %copy-start.11 = (bf16[2,256,1536]{2,1,0:T(8,128)(2,1)S(1)}, bf16[2,256,1536]{2,1,0:T(8,128)(2,1)}, u32[]{:S(2)}) copy-start(bf16[2,256,1536]{2,1,0:T(8,128)(2,1)} %slice_select_fusion) | copy-start | bytes 4718596
  401.4 49.3 %collective-permute-start.9 = (bf16[1536,384]{1,0:T(8,128)(2,1)S(1)}, bf16[1536,384]{1,0:T(8,128)(2,1)S(1)}, u32[]{:S(2)}, u32[]{:S(2)}) collective-permute-start(bf16[1536,384]{1,0:T(8,128)(2,1)S(1)} %broadcast_select_fusion.2), channel_id=1, source_target_pairs={{0,2},{1,3},{2,0},{3,1},{4,6},{5,7},{6,4},{7,5},{8,10},{9,11},{10,... | collective-permute-start | bytes 3538952 | tf_op jit(solution)/shard_map/ppermute | solution.py:1826
  425.3 11.8 %collective-permute-start.17 = (bf16[384,384]{1,0:T(8,128)(2,1)S(1)}, bf16[384,384]{1,0:T(8,128)(2,1)S(1)}, u32[]{:S(2)}, u32[]{:S(2)}) collective-permute-start(bf16[384,384]{1,0:T(8,128)(2,1)S(1)} %get-tuple-element.170), channel_id=1, source_target_pairs={{0,12},{4,0},{8,4},{12,8},{1,13},{5,1},{9,5},{13,9},{2,14},{6,2},{... | collective-permute-start | bytes 884744 | tf_op jit(solution)/shard_map/ppermute | solution.py:1939
  428.6 21.1 %collective-permute-start.16 = (bf16[384,384]{1,0:T(8,128)(2,1)S(1)}, bf16[384,384]{1,0:T(8,128)(2,1)S(1)}, u32[]{:S(2)}, u32[]{:S(2)}) collective-permute-start(bf16[384,384]{1,0:T(8,128)(2,1)S(1)} %get-tuple-element.171), channel_id=1, source_target_pairs={{0,8},{4,12},{8,0},{12,4},{1,9},{5,13},{9,1},{13,5},{2,10},{6,14},... | collective-permute-start | bytes 884744 | tf_op jit(solution)/shard_map/ppermute | solution.py:1939
  428.6 21.1 %collective-permute-start.15 = (bf16[384,384]{1,0:T(8,128)(2,1)S(1)}, bf16[384,384]{1,0:T(8,128)(2,1)S(1)}, u32[]{:S(2)}, u32[]{:S(2)}) collective-permute-start(bf16[384,384]{1,0:T(8,128)(2,1)S(1)} %get-tuple-element.169), channel_id=1, source_target_pairs={{0,4},{4,8},{8,12},{12,0},{1,5},{5,9},{9,13},{13,1},{2,6},{6,10},{... | collective-permute-start | bytes 884744 | tf_op jit(solution)/shard_map/ppermute | solution.py:1939
  437.2 62.6 %collective-permute-start.2 = (bf16[256,1536]{1,0:T(8,128)(2,1)}, bf16[256,1536]{1,0:T(8,128)(2,1)}, u32[]{:S(2)}, u32[]{:S(2)}) collective-permute-start(bf16[256,1536]{1,0:T(8,128)(2,1)} %fusion.10), channel_id=1, source_target_pairs={{0,16},{16,0},{1,17},{17,1},{2,18},{18,2},{3,19},{19,3},{4,20},{20... | collective-permute-start | bytes 2359304 | tf_op jit(solution)/shard_map/ppermute | solution.py:1820
  479.4 11.1 %copy-start.26 = (bf16[1,4,384,768]{3,2,1,0:T(8,128)(2,1)S(1)}, bf16[1,4,384,768]{3,2,1,0:T(8,128)(2,1)}, u32[]{:S(2)}) copy-start(bf16[1,4,384,768]{3,2,1,0:T(8,128)(2,1)} %copy-done.25) | copy-start | bytes 7077892
  479.4 11.1 %copy-start.48 = (bf16[4,256,768]{2,1,0:T(8,128)(2,1)S(1)}, bf16[4,256,768]{2,1,0:T(8,128)(2,1)}, u32[]{:S(2)}) copy-start(bf16[4,256,768]{2,1,0:T(8,128)(2,1)} %get-tuple-element.102) | copy-start | bytes 4718596
  481.4 25.9 %collective-permute-start.6 = (bf16[1024,128]{1,0:T(8,128)(2,1)}, bf16[1024,128]{1,0:T(8,128)(2,1)}, u32[]{:S(2)}, u32[]{:S(2)}) collective-permute-start(bf16[1024,128]{1,0:T(8,128)(2,1)} %broadcast_select_fusion.11), channel_id=1, source_target_pairs={{0,16},{16,0},{1,17},{17,1},{2,18},{18,2},{3,19},{19,3},{4,20},{20... | collective-permute-start | bytes 786440 | tf_op jit(solution)/shard_map/ppermute | solution.py:1820
  482.7 46.6 %collective-permute-start.12 = (bf16[384,896]{1,0:T(8,128)(2,1)}, bf16[384,896]{1,0:T(8,128)(2,1)}, u32[]{:S(2)}, u32[]{:S(2)}) collective-permute-start(bf16[384,896]{1,0:T(8,128)(2,1)} %get-tuple-element.165), channel_id=1, source_target_pairs={{0,12},{4,0},{8,4},{12,8},{1,13},{5,1},{9,5},{13,9},{2,14},{6,2},{... | collective-permute-start | bytes 2064392 | tf_op jit(solution)/shard_map/ppermute | solution.py:1939
  483.8 65.4 %collective-permute-start.11 = (bf16[384,896]{1,0:T(8,128)(2,1)}, bf16[384,896]{1,0:T(8,128)(2,1)}, u32[]{:S(2)}, u32[]{:S(2)}) collective-permute-start(bf16[384,896]{1,0:T(8,128)(2,1)} %get-tuple-element.166), channel_id=1, source_target_pairs={{0,8},{4,12},{8,0},{12,4},{1,9},{5,13},{9,1},{13,5},{2,10},{6,14},... | collective-permute-start | bytes 2064392 | tf_op jit(solution)/shard_map/ppermute | solution.py:1939
  488.5 60.7 %collective-permute-start.10 = (bf16[384,896]{1,0:T(8,128)(2,1)}, bf16[384,896]{1,0:T(8,128)(2,1)}, u32[]{:S(2)}, u32[]{:S(2)}) collective-permute-start(bf16[384,896]{1,0:T(8,128)(2,1)} %get-tuple-element.164), channel_id=1, source_target_pairs={{0,4},{4,8},{8,12},{12,0},{1,5},{5,9},{9,13},{13,1},{2,6},{6,10},{... | collective-permute-start | bytes 2064392 | tf_op jit(solution)/shard_map/ppermute | solution.py:1939
  506.3 10.3 %copy-start.16 = (bf16[4,256,1536]{2,1,0:T(8,128)(2,1)S(1)}, bf16[4,256,1536]{2,1,0:T(8,128)(2,1)}, u32[]{:S(2)}) copy-start(bf16[4,256,1536]{2,1,0:T(8,128)(2,1)} %get-tuple-element.68) | copy-start | bytes 9437188
  508.5 7.9 %collective-permute-start.7 = (bf16[1024,64]{1,0:T(8,128)(2,1)S(1)}, bf16[1024,64]{1,0:T(8,128)(2,1)S(1)}, u32[]{:S(2)}, u32[]{:S(2)}) collective-permute-start(bf16[1024,64]{1,0:T(8,128)(2,1)S(1)} %broadcast_select_fusion.13), channel_id=1, source_target_pairs={{0,1},{1,0},{2,3},{3,2},{4,5},{5,4},{6,7},{7,6},{8,9},{9,8},{10,11... | collective-permute-start | bytes 393224 | tf_op jit(solution)/shard_map/ppermute | solution.py:1823
  516.6 5.8 copy-start.31
  516.6 5.8 copy-start.47
  552.1 152.4 %copy-start.4 = (bf16[4,256,1536]{2,1,0:T(8,128)(2,1)S(1)}, bf16[4,256,1536]{2,1,0:T(8,128)(2,1)}, u32[]{:S(2)}) copy-start(bf16[4,256,1536]{2,1,0:T(8,128)(2,1)} %get-tuple-element.106.cot_all) | copy-start | bytes 9437188
  (19 other events, 44.5 us)
where the time goes:
time: 729 us; the launch traced here: 720 us
  Pallas kernels  452 us (62%)
  matrix products  87.5 us (12%)
  waiting for transfers between devices  74.6 us (10%)
  other arithmetic  45.6 us (6%)
  local copies, waits for them, and re-layouts  33.7 us (5%)
  starting transfers between devices  25.2 us (3%)
    pallas_call x1, Pallas kernels, run_tail(): pl.pallas_call(functools.partial(tail_kernel, ns=ns, ny=ny), in_specs=[VM...  148 us
    pallas_call x1, Pallas kernels, run_start(): pl.pallas_call(functools.partial(start_kernel, ns=ns, ny=ny, taps=taps, h...  87.8 us
    pallas_call x1, Pallas kernels, run_onward(): pl.pallas_call(functools.partial(onward_kernel, inner=inner, ns=ns, ny=ny...  79.5 us
    pallas_call x1, Pallas kernels, run_back(): pl.pallas_call(back_kernel, in_specs=[VM, hbm, hbm, VM, VM, VM], out_spec...  47.3 us
    pallas_call x2, Pallas kernels, run_backward(): pl.pallas_call(functools.partial(backward_kernel, taps=taps, heads=heads)...  47.2 us
    ppermute x6, waiting for transfers between devices, z_sum(): got = lax.ppermute(send, 'shard', [(i, (i + k) % ns) for i in range(ns)])  38.6 us
    dot_general x8, matrix products, dot(): return jnp.dot(a, b, preferred_element_type=F32)  31.8 us
    pallas_call x2, Pallas kernels, run_forward(): pl.pallas_call(functools.partial(forward_kernel, taps=taps, heads=heads,...  24.3 us
  transfers between devices with their start and end apart: 18, of which 6 were waited for; matrix products, arithmetic and copies ran while one was open for 12% of the time, Pallas kernels for 14%

commit v1 on v0

--- a/solution.py
+++ b/solution.py
@@ -301,7 +301,7 @@
     return pl.BlockSpec(dims, lambda i: (0,) * len(dims))
 
 
-PARAMS = pltpu.CompilerParams(dimension_semantics=("arbitrary",), vmem_limit_bytes=60 << 20)
+PARAMS = pltpu.CompilerParams(dimension_semantics=("arbitrary",), vmem_limit_bytes=24 << 20)
 
 
 def run_forward(small, gate, x, bcdt, dmix, taps, heads):
@@ -1219,7 +1219,7 @@
 
 
 PARTS = 2
-PIECE_ROWS = 48
+PIECE_ROWS = 32
 BLOCK = 16
 
 
@@ -1313,7 +1313,8 @@
     lax.fori_loop(0, count, step, 0)
 
 
-def reduce_flow(b, ga_ref, gb_ref, boards, got_ya, acc_a, got_za, own_a, acc_b, got_zb, own_b, ya_s, ya_r, za_s, za_r, zb_s, zb_r, pc_s, pc_r, *, ns, ny):
+def reduce_flow(b, ga_ref, gb_ref, gc_ref, boards, got_ya, acc_a, got_za, own_a, acc_b, got_zb, own_b, acc_c, got_zc, own_c,
+                ya_s, ya_r, za_s, za_r, zb_s, zb_r, zc_s, zc_r, pc_s, pc_r, *, ns, ny):
     _, xb, peer, _ = partners()
     z = lax.axis_index("shard")
     yb = lax.axis_index("rep") // PAIR
@@ -1324,6 +1325,7 @@
         if target not in order:
             order.append(target)
     gather_chip, gather_side, gather_y, gather_x, gather_end = hand_out(b, boards, (own_a, own_b), pc_s, pc_r, ny=ny)
+    chip_c, side_c, y_c, x_c, end_c = hand_out(1 - b, boards, (None, own_c), pc_s, pc_r, ny=ny)
 
     def y_peer(k):
         return {"rep": (yb + k) % ny * PAIR + xb}
@@ -1344,7 +1346,7 @@
         for k in range(1, ny):
             ya(k, z, h).start()
 
-    streams = ((acc_a, got_za, za_s, za_r), (acc_b, got_zb, zb_s, zb_r))
+    streams = ((acc_a, got_za, za_s, za_r), (acc_b, got_zb, zb_s, zb_r), (acc_c, got_zc, zc_s, zc_r))
 
     def line(i, way, target, h):
         acc, got, send, recv = streams[i]
@@ -1360,7 +1362,7 @@
             remote(ga_ref.at[0, target, span_of(h)], got_ya.at[k - 1, target, span_of(h)], ya_s.at[k - 1, target, h],
                    ya_r.at[k - 1, target, h], peer).wait_recv()
 
-    def add(target, h, into_a, into_b, start, extra):
+    def add(target, h, into_a, into_b, into_c, start, extra):
         span = span_of(h)
         total = ga_ref[yb, target, span].astype(F32)
         for k in range(1, ny):
@@ -1368,10 +1370,11 @@
         for place in extra:
             total = total + got_za[place, span].astype(F32)
         into_a[start + (span,)] = total.astype(BF)
-        total = gb_ref[target, span].astype(F32)
-        for place in extra:
-            total = total + got_zb[place, span].astype(F32)
-        into_b[start + (span,)] = total.astype(BF)
+        for ref, got, into in ((gb_ref, got_zb, into_b), (gc_ref, got_zc, into_c)):
+            total = ref[target, span].astype(F32)
+            for place in extra:
+                total = total + got[place, span].astype(F32)
+            into[start + (span,)] = total.astype(BF)
 
     def active(way, target):
         return target > z if way > 0 else target < z
@@ -1382,14 +1385,14 @@
 
         @pl.when(jnp.logical_not(far))
         def _():
-            add(target, h, acc_a, acc_b, (target,), ())
+            add(target, h, acc_a, acc_b, acc_c, (target,), ())
 
         @pl.when(far)
         def _():
             wait_line(target, h)
-            add(target, h, acc_a, acc_b, (target,), (target,))
-
-        for i in range(2):
+            add(target, h, acc_a, acc_b, acc_c, (target,), (target,))
+
+        for i in range(3):
             line(i, way, target, h).start()
 
     def last(h):
@@ -1398,21 +1401,35 @@
         @pl.when(z == 0)
         def _():
             wait_line(ns, h)
-            add(z, h, own_a, own_b, (), (ns,))
+            add(z, h, own_a, own_b, own_c, (), (ns,))
 
         @pl.when(z == ns - 1)
         def _():
             wait_line(z, h)
-            add(z, h, own_a, own_b, (), (z,))
+            add(z, h, own_a, own_b, own_c, (), (z,))
 
         @pl.when((z > 0) & (z < ns - 1))
         def _():
             wait_line(z, h)
             wait_line(ns, h)
-            add(z, h, own_a, own_b, (), (z, ns))
+            add(z, h, own_a, own_b, own_c, (), (z, ns))
 
         for i in range(2):
             gather_chip(i, h)
+        chip_c(1, h)
+
+    def sides(h):
+        for i in range(2):
+            gather_side(i, h)
+        side_c(1, h)
+        for i in range(2):
+            gather_y(i, h)
+        y_c(1, h)
+
+    def crosses(h):
+        for i in range(2):
+            gather_x(i, h)
+        x_c(1, h)
 
     def slot(at):
         for way, target in steps:
@@ -1423,7 +1440,7 @@
                 step(way, target, h)
 
         mine = at - jnp.where(2 * z > ns - 1, z, ns - 1 - z)
-        for late, body in ((0, last), (1, lambda h: [move(i, h) for move in (gather_side, gather_y) for i in range(2)]), (2, lambda h: [gather_x(i, h) for i in range(2)])):
+        for late, body in ((0, last), (1, sides), (2, crosses)):
             @pl.when((mine >= late) & (mine < count + late))
             def _():
                 body(mine - late)
@@ -1432,13 +1449,14 @@
         def ends(h):
             for i in range(2):
                 gather_end(i, h)
+            end_c(1, h)
             for target in range(ns):
                 for k in range(1, ny):
                     ya(k, target, h).wait_send()
             for way, target in steps:
                 @pl.when(active(way, target))
                 def _():
-                    for i in range(2):
+                    for i in range(3):
                         line(i, way, target, h).wait_send()
 
         each(count, ends)
@@ -1457,20 +1475,17 @@
         pltpu.VMEM((ns, ra, ca), BF),
         pltpu.VMEM((ns + 1, ra, ca), BF),
         pltpu.VMEM((ra, ca), BF),
-        pltpu.VMEM((ns, rb, cb), BF),
-        pltpu.VMEM((ns + 1, rb, cb), BF),
-        pltpu.VMEM((rb, cb), BF),
+        *[pltpu.VMEM((ns, rb, cb), BF), pltpu.VMEM((ns + 1, rb, cb), BF), pltpu.VMEM((rb, cb), BF)] * 2,
         dma((ny - 1, ns, parts)), dma((ny - 1, ns, parts)),
-        dma((ns, parts)), dma((ns + 1, parts)),
-        dma((ns, parts)), dma((ns + 1, parts)),
+        *[dma((ns, parts)), dma((ns + 1, parts))] * 3,
         dma((2, ny + 1, PAIR, ny, 2, parts)), dma((2, PAIR, ny, 2, parts)),
     ]
     return outs, scratch
 
 
-def tail_kernel(ga_ref, gb_ref, pa_ref, pb_ref, vec_ref, p_ref, tokens_ref, cot_all, gain_ref,
+def tail_kernel(ga_ref, gb_ref, gc_ref, pa_ref, vec_ref, p_ref, tokens_ref, cot_all, gain_ref,
                 all_a, all_b, vec_out, res_ref, *refs, ns, ny):
-    flow, (got_p, held, got_x, give, rows_ref, cot_ref, vec_y, vec_h, vec_z, vec_t, ra_s, ra_r, v_s, v_r, rows_s) = refs[:15], refs[15:]
+    flow, (got_p, held, got_x, give, rows_ref, cot_ref, vec_y, vec_h, vec_z, vec_t, ra_s, ra_r, v_s, v_r, rows_s) = refs[:20], refs[20:]
     section, xb, peer, beside = partners()
     z = lax.axis_index("shard")
     yb = lax.axis_index("rep") // PAIR
@@ -1512,13 +1527,13 @@
         return remote(give.at[c], res_ref.at[1, pl.ds(c * CHUNK, CHUNK)], ra_s.at[1, 1, c], ra_r.at[1, 1, c], peer)
 
     boards = (all_a, all_b)
-    pieces = flow[13:15]
-    chip1, side1, y1, x1, end1 = hand_out(1, boards, (pa_ref, pb_ref), *pieces, ny=ny)
+    pieces = flow[18:20]
+    chip1, side1, y1, x1, end1 = hand_out(1, boards, (pa_ref, None), *pieces, ny=ny)
     count = ga_ref.shape[2] // PIECE_ROWS
-    start, slot, slots, end0 = reduce_flow(0, ga_ref, gb_ref, boards, *flow, ns=ns, ny=ny)
+    start, slot, slots, end0 = reduce_flow(0, ga_ref, gb_ref, gc_ref, boards, *flow, ns=ns, ny=ny)
 
     def both(body):
-        each(count, lambda h: [body(i, h) for i in (1, 0)])
+        each(count, lambda h: body(0, h))
 
     rows_copy.start()
     cot_copy.start()
@@ -1608,11 +1623,11 @@
             to_side(t).wait_send()
             remote(vec_out.at[t, xb], vec_out.at[t, 1 - xb], v_s.at[ny + ns + t], v_r.at[ny + ns + t], beside).wait_recv()
 
-    ahead = min(3, count)
+    ahead = min(4, count)
     rows_out()
     both(chip1)
     each(ahead, start)
-    between = ((0, pieces_side), (0, rows_beside), (1, sums_z), (3, sums_chip), (4, rows_end), (5, pieces_y), (6, sums_side), (8, sums_end), (10, pieces_x))
+    between = ((0, pieces_side), (0, rows_beside), (1, sums_z), (4, sums_chip), (6, rows_end), (8, pieces_y), (9, sums_side), (12, sums_end), (15, pieces_x))
 
     def go(at, _):
         @pl.when(at + ahead < count)
@@ -1644,7 +1659,7 @@
             p_give(c).wait_recv()
 
 
-def run_tail(ga, gb, pa, pb, vec, p, tokens, cot, gain):
+def run_tail(ga, gb, gc, pa, vec, p, tokens, cot, gain):
     ny, ns = ga.shape[:2]
     seq_len, width = p.shape[1:]
     per = seq_len // CHUNK
@@ -1676,7 +1691,7 @@
         compiler_params=comm_params(4),
         cost_estimate=pl.CostEstimate(flops=50_000_000, bytes_accessed=300_000_000, transcendentals=0),
         name="tail",
-    )(ga, gb, pa, pb, vec, p, tokens, cot, gain)
+    )(ga, gb, gc, pa, vec, p, tokens, cot, gain)
 
 
 def place_kernel(a_ref, b_ref, in_ref, out_ref, dt_ref, *, places, dts, ny):
@@ -1923,7 +1938,9 @@
         cols = [dbc[:, : states2 // 2], dbc[:, states2 // 2 :]]
         total = (pick(s, cols).astype(F32) + swap(pick(s, cols[::-1])).astype(F32)).astype(BF)
         cols = [total[:, : states2 // 4], total[:, states2 // 4 :]]
-        total = (pick(xb, cols).astype(F32) + x_swap(pick(xb, cols[::-1])).astype(F32)).astype(BF)
+        send = pick(xb, cols[::-1])
+        got = x_swap(send)
+        total = (pick(xb, cols).astype(F32) + got.astype(F32)).astype(BF)
         mine = jnp.concatenate([total, dbcdt[:, states2 : states2 + states2 // 4]], axis=1)
         grad_in = [across(normed, jnp.concatenate([v, mine], axis=1)).astype(BF) for v in dparts]
         grad_in = [v.reshape(ns, width // ns, -1) for v in grad_in]
@@ -1962,7 +1979,6 @@
     v1 = out_chip(g_out1, stored1[4], r1)
     gout1 = out_grad(v1)
     d_normed1, gin1, gsmall1 = backward(1, dmix1, stored1, r1, r1 * r1 * r1 * both_sums[seqs * chunks :] / inner)
-    piece_b1 = z_sum(gout1)
     d_normed1, *gin1 = lax.optimization_barrier((d_normed1, *gin1))
     total1 = pick(yb, gin1).astype(F32)
     for k in range(1, ny):
@@ -1992,7 +2008,7 @@
 
     d_normed0, gin0, gsmall0 = backward(0, dmix0, stored0, r0, r0 * r0 * dots0 / inner)
     *pieces, vec, res = run_tail(
-        jnp.stack(gin0), gout0, piece_a1, piece_b1, jnp.stack([gsmall0, gsmall1]), d_normed0, tokens, cot0, gains[0]
+        jnp.stack(gin0), gout0, gout1, piece_a1, jnp.stack([gsmall0, gsmall1]), d_normed0, tokens, cot0, gains[0]
     )
     activations = pick(s, (own_hidden, final))
     input_grads = pick(s, (res, of_own(cot0.reshape(PAIR, micro, seq_len, width))))

time: 729 us -> 713 us (0.978)
  matrix products: 87.5 us -> 75.1 us
  Pallas kernels: 452 us -> 442 us
  local copies, waits for them, and re-layouts: 33.7 us -> 42.4 us
  waiting for transfers between devices: 74.6 us -> 83.1 us
    ppermute x6 -> x3, waiting for transfers between devices: 38.6 us -> 20.1 us  [z_sum(): got = lax.ppermute(send, 'shard', [(i, (i + k) % ns) for i in range(ns)])]
    ppermute x3, waiting for transfers between devices: 13.2 us -> 30.1 us  [x_swap(): return lax.ppermute(v, 'rep', [(i, i ^ 1) for i in range(nr)])]
    unnamed x100 -> x156, local copies, waits for them, and re-layouts: 13 us -> 28.5 us
    dot_general x8, matrix products: 31.8 us -> 21 us  [dot(): return jnp.dot(a, b, preferred_element_type=F32)]
    ppermute x3, waiting for transfers between devices: 22.7 us -> 32.9 us  [y_send(): lax.ppermute(v, 'rep', [(i, (i // PAIR + k) % ny * PAIR + i % PAIR) for i...]
    ppermute x6 -> x3, starting transfers between devices: 11.9 us -> 3.9 us  [z_sum(): got = lax.ppermute(send, 'shard', [(i, (i + k) % ns) for i in range(ns)])]
  transfers between devices with their start and end apart: 18 -> 15, of which waited for: 6 -> 6; matrix products, arithmetic and copies ran while one was open for 12% -> 11% of each run, Pallas kernels for 14% -> 14%
where the time goes in v1:
time: 713 us; the launch traced here: 702 us
  Pallas kernels  442 us (62%)
  waiting for transfers between devices  83.1 us (12%)
  matrix products  75.1 us (11%)
  local copies, waits for them, and re-layouts  42.4 us (6%)
  other arithmetic  39.3 us (6%)
  starting transfers between devices  18 us (3%)
    pallas_call x1, Pallas kernels, run_tail(): pl.pallas_call(functools.partial(tail_kernel, ns=ns, ny=ny), in_specs=[VM...  152 us
    pallas_call x1, Pallas kernels, run_start(): pl.pallas_call(functools.partial(start_kernel, ns=ns, ny=ny, taps=taps, h...  87.9 us
    pallas_call x1, Pallas kernels, run_onward(): pl.pallas_call(functools.partial(onward_kernel, inner=inner, ns=ns, ny=ny...  79.6 us
    pallas_call x1, Pallas kernels, run_back(): pl.pallas_call(back_kernel, in_specs=[VM, hbm, hbm, VM, VM, VM], out_spec...  47.4 us
    pallas_call x2, Pallas kernels, run_backward(): pl.pallas_call(functools.partial(backward_kernel, taps=taps, heads=heads)...  41.9 us
    ppermute x3, waiting for transfers between devices, y_send(): lax.ppermute(v, 'rep', [(i, (i // PAIR + k) % ny * PAIR + i % PAIR) for i...  32.9 us
    ppermute x3, waiting for transfers between devices, x_swap(): return lax.ppermute(v, 'rep', [(i, i ^ 1) for i in range(nr)])  30.1 us
    unnamed x156, local copies, waits for them, and re-layouts  28.5 us
  transfers between devices with their start and end apart: 15, of which 6 were waited for; matrix products, arithmetic and copies ran while one was open for 11% of the time, Pallas kernels for 14%

profile of v1, /device:TPU:0, one launch (start us, length us, event | category | flops | bytes accessed | tf_op | source)
XLA Modules:
  0.0 701.9 jit_solution(4870708661971675043)
XLA Ops:
  4.5 2.8 slice_select_fusion.10
  11.3 87.9 %start.1 = (bf16[2,2,2,256,1536]{4,3,2,1,0:T(8,128)(2,1)}, bf16[4,256,1536]{2,1,0:T(8,128)(2,1)}, bf16[4,256,1536]{2,1,0:T(8,128)(2,1)}, f32[8,128]{1,0:T(8,128)...) custom-call(bf16[2,256,1536]{2,1,0:T(8,128)(2,1)} %bitcast.257, ...), custom_call_target="tpu_custom_call" | custom-call | flops 50000000 | bytes 200000000 | tf_op jit(solution)/shard_map/start/pallas_call | solution.py:963
  101.3 2.8 fusion.36
  104.6 2.6 convolution_convert_fusion.11
  107.2 2.6 convolution_convert_fusion.10
  109.9 1.8 fusion.19.bcdt_ref
  112.4 9.6 %mix_forward.2 = (bf16[4,256,768]{2,1,0:T(8,128)(2,1)S(1)}, bf16[4,256,768]{2,1,0:T(8,128)(2,1)S(1)}, f32[4,1,128,768]{3,2,1,0:T(8,128)S(1)}, f32[4,2,128]{2,1,0:T(2,128)S(1)}) custom-call(f32[8,768]{1,0:T(8,128)S(1)} %get-tuple-element.170.px_ref, f32[8,256]{1,0:T(8,128)S(1)} %get-tuple-element.172.pbc_ref, f32[8,128]{1,0:T(8,128)S(1)} %get-tuple-element.179.ph_ref, ...), custom_call_target="tpu_custom_call" | custom-call | flops 1600000000 | bytes 16000000 | tf_op jit(solution)/shard_map/mix_forward/pallas_call | solution.py:314
  122.6 4.0 convolution_convert_fusion.1
  126.6 79.6 %onward.1 = (bf16[4,256,1536]{2,1,0:T(8,128)(2,1)}, bf16[4,256,1536]{2,1,0:T(8,128)(2,1)}, f32[8,128]{1,0:T(8,128)}, bf16[4,128,1536]{2,1,0:T(8,128)(2,1)}, bf16...) custom-call(bf16[4,256,1536]{2,1,0:T(8,128)(2,1)} %bitcast.246, ...), custom_call_target="tpu_custom_call" | custom-call | flops 50000000 | bytes 150000000 | tf_op jit(solution)/shard_map/onward/pallas_call | solution.py:1183
  206.2 2.8 fusion.35
  212.5 2.6 convolution_convert_fusion.9
  215.2 2.6 convolution_convert_fusion.8
  218.3 2.6 convolution_convert_fusion.7
  221.0 10.0 %mix_forward.3 = (bf16[4,256,768]{2,1,0:T(8,128)(2,1)S(1)}, bf16[4,256,768]{2,1,0:T(8,128)(2,1)S(1)}, f32[4,1,128,768]{3,2,1,0:T(8,128)S(1)}, f32[4,2,128]{2,1,0:T(2,128)S(1)}, f32[4,2,128]{2,1,0:T(2,128)S(1)}) custom-call(f32[8,768]{1,0:T(8,128)S(1)} %get-tuple-element.169.px_ref, f32[8,256]{1,0:T(8,128)S(1)} %get-tuple-element.171.pbc_ref, ...), custom_call_target="tpu_custom_call" | custom-call | flops 1600000000 | bytes 16000000 | tf_op jit(solution)/shard_map/mix_forward/pallas_call | solution.py:314
  231.1 3.0 convolution_convert_fusion
  236.4 6.4 collective-permute-start
  243.3 6.5 token_sums.1
  259.0 21.0 %mix_backward.2 = (bf16[4,256,768]{2,1,0:T(8,128)(2,1)S(1)}, bf16[4,256,768]{2,1,0:T(8,128)(2,1)S(1)}, bf16[4,256,384]{2,1,0:T(8,128)(2,1)S(1)}, f32[8,1152]{1,0:T(8,128)S(1)}) custom-call(f32[8,768]{1,0:T(8,128)S(1)} %get-tuple-element.169.px_ref, f32[8,256]{1,0:T(8,128)S(1)} %get-tuple-element.171.pbc_ref, f32[8,128]{1,0:T(8,128)S(1)} %get-tuple-element.178.ph_ref, ...), custom_call_target="tpu_custom_call" | custom-call | flops 4800000000 | bytes 24000000 | tf_op jit(solution)/shard_map/mix_backward/pallas_call | solution.py:336
  282.5 5.2 bitcast_convert_fusion
  293.6 2.6 fusion.39
  296.3 2.6 fusion.38
  298.9 4.0 multiply_reduce_fusion
  304.3 7.9 %collective-permute-done.4 = bf16[1024,64]{1,0:T(8,128)(2,1)S(1)} collective-permute-done((bf16[1024,64]{1,0:T(8,128)(2,1)S(1)}, bf16[1024,64]{1,0:T(8,128)(2,1)S(1)}, u32[]{:S(2)}, u32[]{:S(2)}) %collective-permute-start.4) | collective-permute-done | bytes 131104 | tf_op jit(solution)/shard_map/ppermute | solution.py:1838
  312.4 6.2 convolution_convert_fusion.5
  318.7 4.3 convolution_convert_fusion.4
  323.0 2.0 broadcast_select_fusion
  326.9 47.4 %back.1 = (bf16[4,256,1536]{2,1,0:T(8,128)(2,1)}, bf16[4,256,1536]{2,1,0:T(8,128)(2,1)}, f32[8,128]{1,0:T(8,128)}) custom-call(bf16[4,256,1536]{2,1,0:T(8,128)(2,1)} %bitcast.224, bf16[4,256,1536]{2,1,0:T(8,128)(2,1)} %get-tuple-element.77.hidden_ref, bf16[2,2,2,256,1536]{4,3,2,1,0:T(8,128)(2,1)} %get-tuple-element.73.tokens_ref, ...), custom_call_target="tpu_custom_call" | custom-call | flops 50000000 | bytes 150000000 | tf_op jit(solution)/shard_map/back/pallas_call | solution.py:1205
  374.3 5.3 bitcast_convert_fusion.1
  381.5 2.6 convolution_convert_fusion.6
  386.4 2.0 fusion
  392.8 15.5 %collective-permute-done.1 = bf16[256,1536]{1,0:T(8,128)(2,1)S(1)} collective-permute-done((bf16[256,1536]{1,0:T(8,128)(2,1)S(1)}, bf16[256,1536]{1,0:T(8,128)(2,1)S(1)}, u32[]{:S(2)}, u32[]{:S(2)}) %collective-permute-start.1) | collective-permute-done | bytes 786464 | tf_op jit(solution)/shard_map/ppermute | solution.py:1838
  409.0 10.1 %collective-permute-done.11 = bf16[1536,384]{1,0:T(8,128)(2,1)S(1)} collective-permute-done((bf16[1536,384]{1,0:T(8,128)(2,1)S(1)}, bf16[1536,384]{1,0:T(8,128)(2,1)S(1)}, u32[]{:S(2)}, u32[]{:S(2)}) %collective-permute-start.11) | collective-permute-done | bytes 1179680 | tf_op jit(solution)/shard_map/ppermute | solution.py:1841
  420.6 22.8 %collective-permute-done.9 = bf16[1536,384]{1,0:T(8,128)(2,1)S(1)} collective-permute-done((bf16[1536,384]{1,0:T(8,128)(2,1)S(1)}, bf16[1536,384]{1,0:T(8,128)(2,1)S(1)}, u32[]{:S(2)}, u32[]{:S(2)}) %collective-permute-start.9) | collective-permute-done | bytes 1179680 | tf_op jit(solution)/shard_map/ppermute | solution.py:1841
  444.9 2.9 add_convert_fusion
  448.5 20.9 %mix_backward.3 = (bf16[4,256,768]{2,1,0:T(8,128)(2,1)S(1)}, bf16[4,256,768]{2,1,0:T(8,128)(2,1)S(1)}, bf16[4,256,384]{2,1,0:T(8,128)(2,1)S(1)}, f32[8,1152]{1,0:T(8,128)S(1)}) custom-call(f32[8,768]{1,0:T(8,128)S(1)} %get-tuple-element.170.px_ref, f32[8,256]{1,0:T(8,128)S(1)} %get-tuple-element.172.pbc_ref, f32[8,128]{1,0:T(8,128)S(1)} %get-tuple-element.179.ph_ref, ...), custom_call_target="tpu_custom_call" | custom-call | flops 4800000000 | bytes 24000000 | tf_op jit(solution)/shard_map/mix_backward/pallas_call | solution.py:336
  471.5 3.1 collective-permute-start.14
  475.4 2.6 fusion.41
  478.1 2.6 fusion.40
  480.8 4.0 fusion.34
  491.1 6.7 collective-permute-done.7
  498.0 5.4 convolution_convert_fusion.2
  503.4 3.9 convolution_convert_fusion.3
  507.4 3.0 pad_maximum_fusion.ga_ref
  510.3 20.1 %collective-permute-done.13 = bf16[384,896]{1,0:T(8,128)(2,1)} collective-permute-done((bf16[384,896]{1,0:T(8,128)(2,1)}, bf16[384,896]{1,0:T(8,128)(2,1)}, u32[]{:S(2)}, u32[]{:S(2)}) %collective-permute-start.13) | collective-permute-done | bytes 688160 | tf_op jit(solution)/shard_map/ppermute | solution.py:1956
  530.4 2.8 fusion.13.pa_ref
  533.2 151.8 %tail.1 = (bf16[2,2,2,384,896]{4,3,2,1,0:T(8,128)(2,1)}, bf16[2,2,2,384,384]{4,3,2,1,0:T(8,128)(2,1)}, f32[2,2,16,1152]{3,2,1,0:T(8,128)}, bf16[2,256,1536]{2,1,0:T(8,128)(2,1)}) custom-call(bf16[2,4,384,896]{3,2,1,0:T(8,128)(2,1)} %pad_maximum_fusion.ga_ref, bf16[4,384,384]{2,1,0:T(8,128)(2,1)} %bitcast.237, bf16[4,384,384]{2,1,0:T(8,128)(2,1)} %bitcast.236, ...), custom_call_target="tpu_custom_call" | custom-call | flops 50000000 | bytes 300000000 | tf_op jit(solution)/shard_map/tail/pallas_call | solution.py:1670
  688.2 3.9 select_bitcast_fusion
  694.5 5.9 place.1
  (237 shorter events, 68.1 us)
Async XLA Ops:
  101.3 3.3 copy-start.49
  111.7 10.3 %copy-start.24 = (f32[4,256,384]{2,1,0:T(8,128)}, f32[4,256,384]{2,1,0:T(8,128)S(1)}, u32[]{:S(2)}) copy-start(f32[4,256,384]{2,1,0:T(8,128)S(1)} %fusion.19.bcdt_ref) | copy-start | bytes 4718596
  112.4 10.2 %copy-start.74 = (bf16[2,2,192,1536]{3,2,1,0:T(8,128)(2,1)S(1)}, bf16[2,2,192,1536]{3,2,1,0:T(8,128)(2,1)}, u32[]{:S(2)}) copy-start(bf16[2,2,192,1536]{3,2,1,0:T(8,128)(2,1)} %get-tuple-element.72) | copy-start | bytes 7077892
  122.6 4.0 copy-start.6
  122.6 4.0 copy-start.32
  122.6 4.0 copy-start.34
  206.2 3.3 copy-start.52
  206.2 4.5 copy-start.56
  209.1 3.5 copy-start.64
  209.1 6.1 copy-start.66
  212.5 8.5 %copy-start.26 = (f32[4,256,384]{2,1,0:T(8,128)}, f32[4,256,384]{2,1,0:T(8,128)S(1)}, u32[]{:S(2)}) copy-start(f32[4,256,384]{2,1,0:T(8,128)S(1)} %fusion.16.bcdt_ref) | copy-start | bytes 4718596
  215.1 5.9 copy-start.18
  221.0 10.1 %copy-start.22 = (bf16[1024,768]{1,0:T(8,128)(2,1)}, bf16[1024,768]{1,0:T(8,128)(2,1)S(1)}, u32[]{:S(2)}) copy-start(bf16[1024,768]{1,0:T(8,128)(2,1)S(1)} %convolution_convert_fusion.7) | copy-start | bytes 4718596
  234.2 15.7 %copy-start.68 = (f32[8,128]{1,0:T(8,128)S(1)}, f32[8,128]{1,0:T(8,128)}, u32[]{:S(2)}) copy-start(f32[8,128]{1,0:T(8,128)} %get-tuple-element.75.live_ref) | copy-start | bytes 12292
  236.4 149.5 %collective-permute-start = (bf16[2,256,1536]{2,1,0:T(8,128)(2,1)}, bf16[2,256,1536]{2,1,0:T(8,128)(2,1)}, u32[]{:S(2)}, u32[]{:S(2)}) collective-permute-start(bf16[2,256,1536]{2,1,0:T(8,128)(2,1)} %select_bitcast_fusion.1), channel_id=1, source_target_pairs={{0,16},{16,0},{1,17},{17,1},{2,18},{18,2},{3,19},{19,3},{4,20},{20... | collective-permute-start | bytes 4718600 | tf_op jit(solution)/shard_map/ppermute | solution.py:1835
  282.4 20.8 %collective-permute-start.3 = (bf16[1024,128]{1,0:T(8,128)(2,1)S(1)}, bf16[1024,128]{1,0:T(8,128)(2,1)S(1)}, u32[]{:S(2)}, u32[]{:S(2)}) collective-permute-start(bf16[1024,128]{1,0:T(8,128)(2,1)S(1)} %broadcast_select_fusion.12), channel_id=1, source_target_pairs={{0,16},{16,0},{1,17},{17,1},{2,18},{18,2},{3,19},{19,3},{4,20},{20... | collective-permute-start | bytes 786440 | tf_op jit(solution)/shard_map/ppermute | solution.py:1835
  288.8 95.4 %collective-permute-start.10 = (bf16[768,768]{1,0:T(8,128)(2,1)}, bf16[768,768]{1,0:T(8,128)(2,1)}, u32[]{:S(2)}, u32[]{:S(2)}) collective-permute-start(bf16[768,768]{1,0:T(8,128)(2,1)} %broadcast_select_fusion.5), channel_id=1, source_target_pairs={{0,16},{16,0},{1,17},{17,1},{2,18},{18,2},{3,19},{19,3},{4,20},{20... | collective-permute-start | bytes 3538952 | tf_op jit(solution)/shard_map/ppermute | solution.py:1835
  298.9 4.1 copy-start.69
  303.1 9.2 %copy-start.13 = (bf16[4,256,768]{2,1,0:T(8,128)(2,1)S(1)}, bf16[4,256,768]{2,1,0:T(8,128)(2,1)}, u32[]{:S(2)}) copy-start(bf16[4,256,768]{2,1,0:T(8,128)(2,1)} %copy-done.11) | copy-start | bytes 4718596
  303.5 8.8 %collective-permute-start.4 = (bf16[1024,64]{1,0:T(8,128)(2,1)S(1)}, bf16[1024,64]{1,0:T(8,128)(2,1)S(1)}, u32[]{:S(2)}, u32[]{:S(2)}) collective-permute-start(bf16[1024,64]{1,0:T(8,128)(2,1)S(1)} %broadcast_select_fusion.14), channel_id=1, source_target_pairs={{0,1},{1,0},{2,3},{3,2},{4,5},{5,4},{6,7},{7,6},{8,9},{9,8},{10,11... | collective-permute-start | bytes 393224 | tf_op jit(solution)/shard_map/ppermute | solution.py:1838
  312.4 6.2 copy-start.10
  312.4 6.2 copy-start.54
  318.6 4.4 copy-start.42
  325.4 119.5 %collective-permute-start.5 = (bf16[4,384,896]{2,1,0:T(8,128)(2,1)}, bf16[4,384,896]{2,1,0:T(8,128)(2,1)}, u32[]{:S(2)}, u32[]{:S(2)}) collective-permute-start(bf16[4,384,896]{2,1,0:T(8,128)(2,1)} %broadcast_select_fusion), channel_id=1, source_target_pairs={{0,2},{1,3},{2,0},{3,1},{4,6},{5,7},{6,4},{7,5},{8,10},{9,11},{10,... | collective-permute-start | bytes 8257544 | tf_op jit(solution)/shard_map/ppermute | solution.py:1841
  326.9 47.4 %copy-start.7 = (bf16[4,256,768]{2,1,0:T(8,128)(2,1)S(1)}, bf16[4,256,768]{2,1,0:T(8,128)(2,1)}, u32[]{:S(2)}) copy-start(bf16[4,256,768]{2,1,0:T(8,128)(2,1)} %copy-done.6) | copy-start | bytes 4718596
  374.3 6.0 copy-start.75
  379.8 10.9 %collective-permute-start.8 = (bf16[768,768]{1,0:T(8,128)(2,1)S(1)}, bf16[768,768]{1,0:T(8,128)(2,1)S(1)}, u32[]{:S(2)}, u32[]{:S(2)}) collective-permute-start(bf16[768,768]{1,0:T(8,128)(2,1)S(1)} %broadcast_select_fusion.9), channel_id=1, source_target_pairs={{0,16},{16,0},{1,17},{17,1},{2,18},{18,2},{3,19},{19,3},{4,20},{20... | collective-permute-start | bytes 3538952 | tf_op jit(solution)/shard_map/ppermute | solution.py:1835
  388.5 19.8 %collective-permute-start.1 = (bf16[256,1536]{1,0:T(8,128)(2,1)S(1)}, bf16[256,1536]{1,0:T(8,128)(2,1)S(1)}, u32[]{:S(2)}, u32[]{:S(2)}) collective-permute-start(bf16[256,1536]{1,0:T(8,128)(2,1)S(1)} %select_bitcast_fusion.4), channel_id=1, source_target_pairs={{0,1},{1,0},{2,3},{3,2},{4,5},{5,4},{6,7},{7,6},{8,9},{9,8},{10,11... | collective-permute-start | bytes 2359304 | tf_op jit(solution)/shard_map/ppermute | solution.py:1838
  390.1 28.9 %collective-permute-start.11 = (bf16[1536,384]{1,0:T(8,128)(2,1)S(1)}, bf16[1536,384]{1,0:T(8,128)(2,1)S(1)}, u32[]{:S(2)}, u32[]{:S(2)}) collective-permute-start(bf16[1536,384]{1,0:T(8,128)(2,1)S(1)} %broadcast_select_fusion.1), channel_id=1, source_target_pairs={{0,2},{1,3},{2,0},{3,1},{4,6},{5,7},{6,4},{7,5},{8,10},{9,11},{10,... | collective-permute-start | bytes 3538952 | tf_op jit(solution)/shard_map/ppermute | solution.py:1841
  390.9 17.4 %copy-start.48 = (bf16[2,256,1536]{2,1,0:T(8,128)(2,1)S(1)}, bf16[2,256,1536]{2,1,0:T(8,128)(2,1)}, u32[]{:S(2)}) copy-start(bf16[2,256,1536]{2,1,0:T(8,128)(2,1)} %slice_select_fusion) | copy-start | bytes 4718596
  391.2 52.1 %collective-permute-start.9 = (bf16[1536,384]{1,0:T(8,128)(2,1)S(1)}, bf16[1536,384]{1,0:T(8,128)(2,1)S(1)}, u32[]{:S(2)}, u32[]{:S(2)}) collective-permute-start(bf16[1536,384]{1,0:T(8,128)(2,1)S(1)} %broadcast_select_fusion.2), channel_id=1, source_target_pairs={{0,2},{1,3},{2,0},{3,1},{4,6},{5,7},{6,4},{7,5},{8,10},{9,11},{10,... | collective-permute-start | bytes 3538952 | tf_op jit(solution)/shard_map/ppermute | solution.py:1841
  408.9 75.9 %collective-permute-start.2 = (bf16[256,1536]{1,0:T(8,128)(2,1)S(1)}, bf16[256,1536]{1,0:T(8,128)(2,1)S(1)}, u32[]{:S(2)}, u32[]{:S(2)}) collective-permute-start(bf16[256,1536]{1,0:T(8,128)(2,1)S(1)} %fusion.10), channel_id=1, source_target_pairs={{0,16},{16,0},{1,17},{17,1},{2,18},{18,2},{3,19},{19,3},{4,20},{20... | collective-permute-start | bytes 2359304 | tf_op jit(solution)/shard_map/ppermute | solution.py:1835
  419.0 25.8 %copy-start.45 = (bf16[1536,896]{1,0:T(8,128)(2,1)S(1)}, bf16[1536,896]{1,0:T(8,128)(2,1)}, u32[]{:S(2)}) copy-start(bf16[1536,896]{1,0:T(8,128)(2,1)} %copy-done.44) | copy-start | bytes 8257540
  420.6 24.3 %copy-start.43 = (bf16[1536,896]{1,0:T(8,128)(2,1)S(1)}, bf16[1536,896]{1,0:T(8,128)(2,1)}, u32[]{:S(2)}) copy-start(bf16[1536,896]{1,0:T(8,128)(2,1)} %copy-done.42) | copy-start | bytes 8257540
  444.8 3.7 copy-start.35
  447.8 22.4 %copy-start.38 = (bf16[4,384,896]{2,1,0:T(8,128)(2,1)}, bf16[4,384,896]{2,1,0:T(8,128)(2,1)S(1)}, u32[]{:S(2)}) copy-start(bf16[4,384,896]{2,1,0:T(8,128)(2,1)S(1)} %add_convert_fusion) | copy-start | bytes 8257540
  469.4 6.0 copy-start.16
  469.4 8.7 %copy-start.14 = (bf16[4,256,768]{2,1,0:T(8,128)(2,1)}, bf16[4,256,768]{2,1,0:T(8,128)(2,1)S(1)}, u32[]{:S(2)}) copy-start(bf16[4,256,768]{2,1,0:T(8,128)(2,1)S(1)} %get-tuple-element.100) | copy-start | bytes 4718596
  469.4 6.0 copy-start.63
  470.1 18.1 %collective-permute-start.6 = (bf16[1024,128]{1,0:T(8,128)(2,1)}, bf16[1024,128]{1,0:T(8,128)(2,1)}, u32[]{:S(2)}, u32[]{:S(2)}) collective-permute-start(bf16[1024,128]{1,0:T(8,128)(2,1)} %broadcast_select_fusion.11), channel_id=1, source_target_pairs={{0,16},{16,0},{1,17},{17,1},{2,18},{18,2},{3,19},{19,3},{4,20},{20... | collective-permute-start | bytes 786440 | tf_op jit(solution)/shard_map/ppermute | solution.py:1835
  471.5 38.8 %collective-permute-start.14 = (bf16[384,896]{1,0:T(8,128)(2,1)}, bf16[384,896]{1,0:T(8,128)(2,1)S(1)}, u32[]{:S(2)}, u32[]{:S(2)}) collective-permute-start(bf16[384,896]{1,0:T(8,128)(2,1)} %get-tuple-element.165), channel_id=1, source_target_pairs={{0,12},{4,0},{8,4},{12,8},{1,13},{5,1},{9,5},{13,9},{2,14},{6,2},{... | collective-permute-start | bytes 2064392 | tf_op jit(solution)/shard_map/ppermute | solution.py:1956
  474.7 55.8 %collective-permute-start.13 = (bf16[384,896]{1,0:T(8,128)(2,1)}, bf16[384,896]{1,0:T(8,128)(2,1)}, u32[]{:S(2)}, u32[]{:S(2)}) collective-permute-start(bf16[384,896]{1,0:T(8,128)(2,1)} %get-tuple-element.166), channel_id=1, source_target_pairs={{0,8},{4,12},{8,0},{12,4},{1,9},{5,13},{9,1},{13,5},{2,10},{6,14},... | collective-permute-start | bytes 2064392 | tf_op jit(solution)/shard_map/ppermute | solution.py:1956
  474.7 55.8 %collective-permute-start.12 = (bf16[384,896]{1,0:T(8,128)(2,1)}, bf16[384,896]{1,0:T(8,128)(2,1)}, u32[]{:S(2)}, u32[]{:S(2)}) collective-permute-start(bf16[384,896]{1,0:T(8,128)(2,1)} %get-tuple-element.164), channel_id=1, source_target_pairs={{0,4},{4,8},{8,12},{12,0},{1,5},{5,9},{9,13},{13,1},{2,6},{6,10},{... | collective-permute-start | bytes 2064392 | tf_op jit(solution)/shard_map/ppermute | solution.py:1956
  488.2 9.8 %copy-start.51 = (bf16[4,256,1536]{2,1,0:T(8,128)(2,1)S(1)}, bf16[4,256,1536]{2,1,0:T(8,128)(2,1)}, u32[]{:S(2)}) copy-start(bf16[4,256,1536]{2,1,0:T(8,128)(2,1)} %get-tuple-element.68) | copy-start | bytes 9437188
  489.6 8.2 %collective-permute-start.7 = (bf16[1024,64]{1,0:T(8,128)(2,1)S(1)}, bf16[1024,64]{1,0:T(8,128)(2,1)S(1)}, u32[]{:S(2)}, u32[]{:S(2)}) collective-permute-start(bf16[1024,64]{1,0:T(8,128)(2,1)S(1)} %broadcast_select_fusion.13), channel_id=1, source_target_pairs={{0,1},{1,0},{2,3},{3,2},{4,5},{5,4},{6,7},{7,6},{8,9},{9,8},{10,11... | collective-permute-start | bytes 393224 | tf_op jit(solution)/shard_map/ppermute | solution.py:1838
  498.0 5.4 copy-start.15
  507.3 23.1 %copy-start.39 = (bf16[4,384,896]{2,1,0:T(8,128)(2,1)S(1)}, bf16[4,384,896]{2,1,0:T(8,128)(2,1)}, u32[]{:S(2)}) copy-start(bf16[4,384,896]{2,1,0:T(8,128)(2,1)} %copy-done.38) | copy-start | bytes 8257540
  688.2 4.5 copy-start
  (44 other events, 99.9 us)

commit v2 on v1

--- a/solution.py
+++ b/solution.py
@@ -301,7 +301,7 @@
     return pl.BlockSpec(dims, lambda i: (0,) * len(dims))
 
 
-PARAMS = pltpu.CompilerParams(dimension_semantics=("arbitrary",), vmem_limit_bytes=24 << 20)
+PARAMS = pltpu.CompilerParams(dimension_semantics=("arbitrary",), vmem_limit_bytes=18 << 20)
 
 
 def run_forward(small, gate, x, bcdt, dmix, taps, heads):
@@ -395,7 +395,7 @@
         out_specs=VM,
         out_shape=jax.ShapeDtypeStruct(v.shape, F32),
         scratch_shapes=[pltpu.VMEM((2,) + v.shape, F32), pltpu.VMEM(v.shape, F32), pltpu.SemaphoreType.DMA((2,)), pltpu.SemaphoreType.DMA((2,))],
-        compiler_params=pltpu.CompilerParams(collective_id=collective_id, has_side_effects=True),
+        compiler_params=comm_params(collective_id, 8),
         cost_estimate=pl.CostEstimate(flops=10_000_000, bytes_accessed=20_000_000, transcendentals=0),
         name="token_sums",
     )(v)
@@ -990,7 +990,7 @@
             dma((3, 2)), dma((2, PAIR, 2)), dma((2 + ny, max(ns, 2), ny)), dma((2, ns, ny)),
             dma((2, ns)), dma((2, ns)), dma(()), dma(()),
         ],
-        compiler_params=comm_params(5),
+        compiler_params=comm_params(5, 34),
         cost_estimate=pl.CostEstimate(flops=50_000_000, bytes_accessed=200_000_000, transcendentals=0),
         name="start",
     )(tokens, counts, *smalls, bc, dt, q, o)
@@ -1170,8 +1170,8 @@
     return pltpu.VMEM((PAIR,) + part.shape[1:], BF)
 
 
-def comm_params(collective_id):
-    return pltpu.CompilerParams(collective_id=collective_id, has_side_effects=True, vmem_limit_bytes=60 << 20)
+def comm_params(collective_id, mib=60):
+    return pltpu.CompilerParams(collective_id=collective_id, has_side_effects=True, vmem_limit_bytes=mib << 20)
 
 
 def run_onward(part, rows, sums, live, gain, q, o, inner, ns):
@@ -1192,7 +1192,7 @@
         ]
         + outs,
         scratch_shapes=wide + [pltpu.VMEM((2,) + sums.shape, F32), small, own_rows(part)] + sems + [pltpu.SemaphoreType.DMA((2,))] * 3 + more,
-        compiler_params=comm_params(1),
+        compiler_params=comm_params(1, 32),
         cost_estimate=pl.CostEstimate(flops=50_000_000, bytes_accessed=150_000_000, transcendentals=0),
         name="onward",
     )(part, rows, sums, live, gain, q, o)
@@ -1212,7 +1212,7 @@
             jax.ShapeDtypeStruct(live.shape, F32),
         ],
         scratch_shapes=wide + [small, small, own_rows(part), own_rows(part)] + sems + [pltpu.SemaphoreType.DMA((2,))] * 4,
-        compiler_params=comm_params(2),
+        compiler_params=comm_params(2, 28),
         cost_estimate=pl.CostEstimate(flops=50_000_000, bytes_accessed=150_000_000, transcendentals=0),
         name="back",
     )(part, hidden, tokens, gained, live, gain)
@@ -1688,7 +1688,7 @@
             dma((ny + ns + 2,)), dma((ny + ns + 2,)),
             dma((2,)),
         ],
-        compiler_params=comm_params(4),
+        compiler_params=comm_params(4, 58),
         cost_estimate=pl.CostEstimate(flops=50_000_000, bytes_accessed=300_000_000, transcendentals=0),
         name="tail",
     )(ga, gb, gc, pa, vec, p, tokens, cot, gain)

time: 713 us -> 682 us (0.957)
  Pallas kernels: 442 us -> 425 us
  local copies, waits for them, and re-layouts: 42.4 us -> 32.8 us
    unnamed x156 -> x148, local copies, waits for them, and re-layouts: 28.5 us -> 20.1 us
where the time goes in v2:
time: 682 us; the launch traced here: 671 us
  Pallas kernels  425 us (62%)
  waiting for transfers between devices  85.4 us (13%)
  matrix products  71.9 us (11%)
  other arithmetic  35.2 us (5%)
  local copies, waits for them, and re-layouts  32.8 us (5%)
  starting transfers between devices  18.5 us (3%)
    pallas_call x1, Pallas kernels, run_tail(): pl.pallas_call(functools.partial(tail_kernel, ns=ns, ny=ny), in_specs=[VM...  152 us
    pallas_call x1, Pallas kernels, run_start(): pl.pallas_call(functools.partial(start_kernel, ns=ns, ny=ny, taps=taps, h...  82.6 us
    pallas_call x1, Pallas kernels, run_onward(): pl.pallas_call(functools.partial(onward_kernel, inner=inner, ns=ns, ny=ny...  72.7 us
    pallas_call x1, Pallas kernels, run_back(): pl.pallas_call(back_kernel, in_specs=[VM, hbm, hbm, VM, VM, VM], out_spec...  42.3 us
    pallas_call x2, Pallas kernels, run_backward(): pl.pallas_call(functools.partial(backward_kernel, taps=taps, heads=heads)...  42.1 us
    ppermute x3, waiting for transfers between devices, y_send(): lax.ppermute(v, 'rep', [(i, (i // PAIR + k) % ny * PAIR + i % PAIR) for i...  34.1 us
    ppermute x3, waiting for transfers between devices, x_swap(): return lax.ppermute(v, 'rep', [(i, i ^ 1) for i in range(nr)])  30.5 us
    ppermute x3, waiting for transfers between devices, z_sum(): got = lax.ppermute(send, 'shard', [(i, (i + k) % ns) for i in range(ns)])  20.7 us
  transfers between devices with their start and end apart: 15, of which 6 were waited for; matrix products, arithmetic and copies ran while one was open for 11% of the time, Pallas kernels for 14%

profile of v2, /device:TPU:0, one launch (start us, length us, event | category | flops | bytes accessed | tf_op | source)
XLA Modules:
  0.0 671.0 jit_solution(3810604213785936957)
XLA Ops:
  3.2 2.8 slice_select_fusion.10
  8.1 82.6 %start.1 = (bf16[2,2,2,256,1536]{4,3,2,1,0:T(8,128)(2,1)}, bf16[4,256,1536]{2,1,0:T(8,128)(2,1)S(1)}, bf16[4,256,1536]{2,1,0:T(8,128)(2,1)S(1)}, f32[8,128]{1,0:...) custom-call(bf16[2,256,1536]{2,1,0:T(8,128)(2,1)S(1)} %bitcast.213, ...), custom_call_target="tpu_custom_call" | custom-call | flops 50000000 | bytes 200000000 | tf_op jit(solution)/shard_map/start/pallas_call | solution.py:963
  90.7 6.1 fusion.36
  96.9 2.6 convolution_convert_fusion.11
  99.5 2.6 convolution_convert_fusion.10
  102.1 1.8 fusion.19.bcdt_ref
  104.6 9.6 %mix_forward.2 = (bf16[4,256,768]{2,1,0:T(8,128)(2,1)S(1)}, bf16[4,256,768]{2,1,0:T(8,128)(2,1)S(1)}, f32[4,1,128,768]{3,2,1,0:T(8,128)S(1)}, f32[4,2,128]{2,1,0:T(2,128)S(1)}) custom-call(f32[8,768]{1,0:T(8,128)S(1)} %get-tuple-element.170.px_ref, f32[8,256]{1,0:T(8,128)S(1)} %get-tuple-element.172.pbc_ref, f32[8,128]{1,0:T(8,128)S(1)} %get-tuple-element.179.ph_ref, ...), custom_call_target="tpu_custom_call" | custom-call | flops 1600000000 | bytes 16000000 | tf_op jit(solution)/shard_map/mix_forward/pallas_call | solution.py:314
  116.6 2.8 convolution_convert_fusion.1
  119.5 72.7 %onward.1 = (bf16[4,256,1536]{2,1,0:T(8,128)(2,1)S(1)}, bf16[4,256,1536]{2,1,0:T(8,128)(2,1)S(1)}, f32[8,128]{1,0:T(8,128)S(1)}, bf16[4,128,1536]{2,1,0:T(8,128)...) custom-call(bf16[4,256,1536]{2,1,0:T(8,128)(2,1)S(1)} %bitcast.212, ...), custom_call_target="tpu_custom_call" | custom-call | flops 50000000 | bytes 150000000 | tf_op jit(solution)/shard_map/onward/pallas_call | solution.py:1183
  193.4 1.8 fusion.16.bcdt_ref
  195.2 2.6 convolution_convert_fusion.9
  197.8 2.6 convolution_convert_fusion.8
  200.4 2.6 convolution_convert_fusion.7
  203.1 10.1 %mix_forward.3 = (bf16[4,256,768]{2,1,0:T(8,128)(2,1)S(1)}, bf16[4,256,768]{2,1,0:T(8,128)(2,1)S(1)}, f32[4,1,128,768]{3,2,1,0:T(8,128)S(1)}, f32[4,2,128]{2,1,0:T(2,128)S(1)}, f32[4,2,128]{2,1,0:T(2,128)S(1)}) custom-call(f32[8,768]{1,0:T(8,128)S(1)} %get-tuple-element.169.px_ref, f32[8,256]{1,0:T(8,128)S(1)} %get-tuple-element.171.pbc_ref, ...), custom_call_target="tpu_custom_call" | custom-call | flops 1600000000 | bytes 16000000 | tf_op jit(solution)/shard_map/mix_forward/pallas_call | solution.py:314
  213.2 3.0 convolution_convert_fusion
  218.4 6.8 %collective-permute-start = (bf16[2,256,1536]{2,1,0:T(8,128)(2,1)}, bf16[2,256,1536]{2,1,0:T(8,128)(2,1)}, u32[]{:S(2)}, u32[]{:S(2)}) collective-permute-start(bf16[2,256,1536]{2,1,0:T(8,128)(2,1)} %select_bitcast_fusion.1), channel_id=1, source_target_pairs={{0,16},{16,0},{1,17},{17,1},{2,18},{18,2},{3,19},{19,3},{4,20},{20... | collective-permute-start | bytes 4718600 | tf_op jit(solution)/shard_map/ppermute | solution.py:1835
  225.2 6.5 token_sums.1
  231.8 21.0 %mix_backward.2 = (bf16[4,256,768]{2,1,0:T(8,128)(2,1)S(1)}, bf16[4,256,768]{2,1,0:T(8,128)(2,1)S(1)}, bf16[4,256,384]{2,1,0:T(8,128)(2,1)S(1)}, f32[8,1152]{1,0:T(8,128)S(1)}) custom-call(f32[8,768]{1,0:T(8,128)S(1)} %get-tuple-element.169.px_ref, f32[8,256]{1,0:T(8,128)S(1)} %get-tuple-element.171.pbc_ref, f32[8,128]{1,0:T(8,128)S(1)} %get-tuple-element.178.ph_ref, ...), custom_call_target="tpu_custom_call" | custom-call | flops 4800000000 | bytes 24000000 | tf_op jit(solution)/shard_map/mix_backward/pallas_call | solution.py:336
  256.8 5.2 bitcast_convert_fusion
  266.5 2.6 fusion.39
  269.2 2.6 fusion.38
  272.0 3.9 multiply_reduce_fusion
  278.9 8.2 %collective-permute-done.4 = bf16[1024,64]{1,0:T(8,128)(2,1)S(1)} collective-permute-done((bf16[1024,64]{1,0:T(8,128)(2,1)S(1)}, bf16[1024,64]{1,0:T(8,128)(2,1)S(1)}, u32[]{:S(2)}, u32[]{:S(2)}) %collective-permute-start.4) | collective-permute-done | bytes 131104 | tf_op jit(solution)/shard_map/ppermute | solution.py:1838
  287.3 6.2 convolution_convert_fusion.5
  293.5 4.3 convolution_convert_fusion.4
  297.9 1.8 broadcast_select_fusion
  301.2 42.3 %back.1 = (bf16[4,256,1536]{2,1,0:T(8,128)(2,1)S(1)}, bf16[4,256,1536]{2,1,0:T(8,128)(2,1)S(1)}, f32[8,128]{1,0:T(8,128)S(1)}) custom-call(bf16[4,256,1536]{2,1,0:T(8,128)(2,1)S(1)} %bitcast.193, bf16[4,256,1536]{2,1,0:T(8,128)(2,1)S(1)} %get-tuple-element.77.hidden_ref, bf16[2,2,2,256,1536]{4,3,2,1,0:T(8,128)(2,1)S(1)} %bitcast.190, ...), custom_call_target="tpu_custom_call" | custom-call | flops 50000000 | bytes 150000000 | tf_op jit(solution)/shard_map/back/pallas_call | solution.py:1205
  343.6 3.4 bitcast_convert_fusion.1
  348.6 2.6 convolution_convert_fusion.6
  353.5 2.0 fusion
  360.0 15.4 %collective-permute-done.1 = bf16[256,1536]{1,0:T(8,128)(2,1)S(1)} collective-permute-done((bf16[256,1536]{1,0:T(8,128)(2,1)S(1)}, bf16[256,1536]{1,0:T(8,128)(2,1)S(1)}, u32[]{:S(2)}, u32[]{:S(2)}) %collective-permute-start.1) | collective-permute-done | bytes 786464 | tf_op jit(solution)/shard_map/ppermute | solution.py:1838
  376.0 11.7 %collective-permute-done.11 = bf16[1536,384]{1,0:T(8,128)(2,1)S(1)} collective-permute-done((bf16[1536,384]{1,0:T(8,128)(2,1)S(1)}, bf16[1536,384]{1,0:T(8,128)(2,1)S(1)}, u32[]{:S(2)}, u32[]{:S(2)}) %collective-permute-start.11) | collective-permute-done | bytes 1179680 | tf_op jit(solution)/shard_map/ppermute | solution.py:1841
  389.2 22.5 %collective-permute-done.9 = bf16[1536,384]{1,0:T(8,128)(2,1)S(1)} collective-permute-done((bf16[1536,384]{1,0:T(8,128)(2,1)S(1)}, bf16[1536,384]{1,0:T(8,128)(2,1)S(1)}, u32[]{:S(2)}, u32[]{:S(2)}) %collective-permute-start.9) | collective-permute-done | bytes 1179680 | tf_op jit(solution)/shard_map/ppermute | solution.py:1841
  417.4 21.1 %mix_backward.3 = (bf16[4,256,768]{2,1,0:T(8,128)(2,1)S(1)}, bf16[4,256,768]{2,1,0:T(8,128)(2,1)S(1)}, bf16[4,256,384]{2,1,0:T(8,128)(2,1)S(1)}, f32[8,1152]{1,0:T(8,128)S(1)}) custom-call(f32[8,768]{1,0:T(8,128)S(1)} %get-tuple-element.170.px_ref, f32[8,256]{1,0:T(8,128)S(1)} %get-tuple-element.172.pbc_ref, f32[8,128]{1,0:T(8,128)S(1)} %get-tuple-element.179.ph_ref, ...), custom_call_target="tpu_custom_call" | custom-call | flops 4800000000 | bytes 24000000 | tf_op jit(solution)/shard_map/mix_backward/pallas_call | solution.py:336
  440.6 3.7 collective-permute-start.14
  445.0 2.6 fusion.41
  447.7 2.6 fusion.40
  450.4 4.0 fusion.34
  459.6 7.0 %collective-permute-done.7 = bf16[1024,64]{1,0:T(8,128)(2,1)S(1)} collective-permute-done((bf16[1024,64]{1,0:T(8,128)(2,1)S(1)}, bf16[1024,64]{1,0:T(8,128)(2,1)S(1)}, u32[]{:S(2)}, u32[]{:S(2)}) %collective-permute-start.7) | collective-permute-done | bytes 131104 | tf_op jit(solution)/shard_map/ppermute | solution.py:1838
  466.8 5.4 convolution_convert_fusion.2
  472.3 3.9 convolution_convert_fusion.3
  476.2 3.0 pad_maximum_fusion.ga_ref
  479.2 20.7 %collective-permute-done.13 = bf16[384,896]{1,0:T(8,128)(2,1)} collective-permute-done((bf16[384,896]{1,0:T(8,128)(2,1)}, bf16[384,896]{1,0:T(8,128)(2,1)}, u32[]{:S(2)}, u32[]{:S(2)}) %collective-permute-start.13) | collective-permute-done | bytes 688160 | tf_op jit(solution)/shard_map/ppermute | solution.py:1956
  499.9 3.0 fusion.13.pa_ref
  502.8 152.3 %tail.1 = (bf16[2,2,2,384,896]{4,3,2,1,0:T(8,128)(2,1)}, bf16[2,2,2,384,384]{4,3,2,1,0:T(8,128)(2,1)}, f32[2,2,16,1152]{3,2,1,0:T(8,128)}, bf16[2,256,1536]{2,1,0:T(8,128)(2,1)}) custom-call(bf16[2,4,384,896]{3,2,1,0:T(8,128)(2,1)} %pad_maximum_fusion.ga_ref, bf16[4,384,384]{2,1,0:T(8,128)(2,1)} %bitcast.258, bf16[4,384,384]{2,1,0:T(8,128)(2,1)} %bitcast.257, ...), custom_call_target="tpu_custom_call" | custom-call | flops 50000000 | bytes 300000000 | tf_op jit(solution)/shard_map/tail/pallas_call | solution.py:1670
  658.3 2.9 select_bitcast_fusion
  661.9 1.7 copy-done.16
  663.6 5.9 place.1
  (230 shorter events, 53.9 us)
Async XLA Ops:
  3.2 3.1 copy-start.60
  90.7 11.5 %copy-start.7 = (bf16[4,256,1536]{2,1,0:T(8,128)(2,1)}, bf16[4,256,1536]{2,1,0:T(8,128)(2,1)S(1)}, u32[]{:S(2)}) copy-start(bf16[4,256,1536]{2,1,0:T(8,128)(2,1)S(1)} %get-tuple-element.68) | copy-start | bytes 9437188
  90.7 26.0 %copy-start.29 = (bf16[2,2,192,1536]{3,2,1,0:T(8,128)(2,1)}, bf16[2,2,192,1536]{3,2,1,0:T(8,128)(2,1)S(1)}, u32[]{:S(2)}) copy-start(bf16[2,2,192,1536]{3,2,1,0:T(8,128)(2,1)S(1)} %get-tuple-element.72) | copy-start | bytes 7077892
  90.7 102.7 %copy-start.13 = (bf16[2,1536,384]{2,1,0:T(8,128)(2,1)}, bf16[2,1536,384]{2,1,0:T(8,128)(2,1)S(1)}, u32[]{:S(2)}) copy-start(bf16[2,1536,384]{2,1,0:T(8,128)(2,1)S(1)} %get-tuple-element.70) | copy-start | bytes 7077892
  90.7 109.7 %copy-start.28 = (bf16[4,256,1536]{2,1,0:T(8,128)(2,1)}, bf16[4,256,1536]{2,1,0:T(8,128)(2,1)S(1)}, u32[]{:S(2)}) copy-start(bf16[4,256,1536]{2,1,0:T(8,128)(2,1)S(1)} %get-tuple-element.80) | copy-start | bytes 9437188
  99.5 5.1 copy-start.31
  103.9 10.3 %copy-start.47 = (f32[4,256,384]{2,1,0:T(8,128)}, f32[4,256,384]{2,1,0:T(8,128)S(1)}, u32[]{:S(2)}) copy-start(f32[4,256,384]{2,1,0:T(8,128)S(1)} %fusion.19.bcdt_ref) | copy-start | bytes 4718596
  192.2 5.6 copy-start.10
  193.4 4.4 copy-start.67
  218.4 134.5 %collective-permute-start = (bf16[2,256,1536]{2,1,0:T(8,128)(2,1)}, bf16[2,256,1536]{2,1,0:T(8,128)(2,1)}, u32[]{:S(2)}, u32[]{:S(2)}) collective-permute-start(bf16[2,256,1536]{2,1,0:T(8,128)(2,1)} %select_bitcast_fusion.1), channel_id=1, source_target_pairs={{0,16},{16,0},{1,17},{17,1},{2,18},{18,2},{3,19},{19,3},{4,20},{20... | collective-permute-start | bytes 4718600 | tf_op jit(solution)/shard_map/ppermute | solution.py:1835
  256.8 19.9 %collective-permute-start.3 = (bf16[1024,128]{1,0:T(8,128)(2,1)}, bf16[1024,128]{1,0:T(8,128)(2,1)}, u32[]{:S(2)}, u32[]{:S(2)}) collective-permute-start(bf16[1024,128]{1,0:T(8,128)(2,1)} %broadcast_select_fusion.12), channel_id=1, source_target_pairs={{0,16},{16,0},{1,17},{17,1},{2,18},{18,2},{3,19},{19,3},{4,20},{20... | collective-permute-start | bytes 786440 | tf_op jit(solution)/shard_map/ppermute | solution.py:1835
  263.3 88.0 %collective-permute-start.10 = (bf16[768,768]{1,0:T(8,128)(2,1)}, bf16[768,768]{1,0:T(8,128)(2,1)}, u32[]{:S(2)}, u32[]{:S(2)}) collective-permute-start(bf16[768,768]{1,0:T(8,128)(2,1)} %broadcast_select_fusion.5), channel_id=1, source_target_pairs={{0,16},{16,0},{1,17},{17,1},{2,18},{18,2},{3,19},{19,3},{4,20},{20... | collective-permute-start | bytes 3538952 | tf_op jit(solution)/shard_map/ppermute | solution.py:1835
  276.7 10.5 %copy-start.42 = (bf16[4,256,768]{2,1,0:T(8,128)(2,1)S(1)}, bf16[4,256,768]{2,1,0:T(8,128)(2,1)}, u32[]{:S(2)}) copy-start(bf16[4,256,768]{2,1,0:T(8,128)(2,1)} %copy-done.40) | copy-start | bytes 4718596
  276.7 10.5 %copy-start.69 = (bf16[1024,64]{1,0:T(8,128)(2,1)S(1)}, bf16[1024,64]{1,0:T(8,128)(2,1)}, u32[]{:S(2)}) copy-start(bf16[1024,64]{1,0:T(8,128)(2,1)} %slice.366) | copy-start | bytes 393220
  278.3 8.8 %collective-permute-start.4 = (bf16[1024,64]{1,0:T(8,128)(2,1)S(1)}, bf16[1024,64]{1,0:T(8,128)(2,1)S(1)}, u32[]{:S(2)}, u32[]{:S(2)}) collective-permute-start(bf16[1024,64]{1,0:T(8,128)(2,1)S(1)} %broadcast_select_fusion.14), channel_id=1, source_target_pairs={{0,1},{1,0},{2,3},{3,2},{4,5},{5,4},{6,7},{7,6},{8,9},{9,8},{10,11... | collective-permute-start | bytes 393224 | tf_op jit(solution)/shard_map/ppermute | solution.py:1838
  287.2 6.2 copy-start.12
  287.3 6.2 copy-start.39
  287.3 13.9 %slice-start = ((s8[6291456]{0:T(1024)(128)(4,1)}), s8[4194304]{0:T(1024)(128)(4,1)S(1)}, s32[]{:S(2)}) async-start(s8[6291456]{0:T(1024)(128)(4,1)} %bitcast.189), calls=%async_computation | async-start | bytes 8388608
  293.5 7.7 %slice-start.1 = ((s8[6291456]{0:T(1024)(128)(4,1)}), s8[2097152]{0:T(1024)(128)(4,1)S(1)}, s32[]{:S(2)}) async-start(s8[6291456]{0:T(1024)(128)(4,1)} %bitcast.189), calls=%async_computation.1 | async-start | bytes 4194304
  297.8 3.4 copy-start
  297.8 3.4 copy-start.18
  299.7 113.4 %collective-permute-start.5 = (bf16[4,384,896]{2,1,0:T(8,128)(2,1)}, bf16[4,384,896]{2,1,0:T(8,128)(2,1)S(1)}, u32[]{:S(2)}, u32[]{:S(2)}) collective-permute-start(bf16[4,384,896]{2,1,0:T(8,128)(2,1)} %broadcast_select_fusion), channel_id=1, source_target_pairs={{0,2},{1,3},{2,0},{3,1},{4,6},{5,7},{6,4},{7,5},{8,10},{9,11},{10,... | collective-permute-start | bytes 8257544 | tf_op jit(solution)/shard_map/ppermute | solution.py:1841
  301.2 42.3 %copy-start.36 = (bf16[4,256,768]{2,1,0:T(8,128)(2,1)S(1)}, bf16[4,256,768]{2,1,0:T(8,128)(2,1)}, u32[]{:S(2)}) copy-start(bf16[4,256,768]{2,1,0:T(8,128)(2,1)} %copy-done.35) | copy-start | bytes 4718596
  343.5 3.4 copy-start.1
  347.1 11.7 %collective-permute-start.8 = (bf16[768,768]{1,0:T(8,128)(2,1)S(1)}, bf16[768,768]{1,0:T(8,128)(2,1)S(1)}, u32[]{:S(2)}, u32[]{:S(2)}) collective-permute-start(bf16[768,768]{1,0:T(8,128)(2,1)S(1)} %broadcast_select_fusion.9), channel_id=1, source_target_pairs={{0,16},{16,0},{1,17},{17,1},{2,18},{18,2},{3,19},{19,3},{4,20},{20... | collective-permute-start | bytes 3538952 | tf_op jit(solution)/shard_map/ppermute | solution.py:1835
  355.5 19.9 %collective-permute-start.1 = (bf16[256,1536]{1,0:T(8,128)(2,1)S(1)}, bf16[256,1536]{1,0:T(8,128)(2,1)S(1)}, u32[]{:S(2)}, u32[]{:S(2)}) collective-permute-start(bf16[256,1536]{1,0:T(8,128)(2,1)S(1)} %select_bitcast_fusion.4), channel_id=1, source_target_pairs={{0,1},{1,0},{2,3},{3,2},{4,5},{5,4},{6,7},{7,6},{8,9},{9,8},{10,11... | collective-permute-start | bytes 2359304 | tf_op jit(solution)/shard_map/ppermute | solution.py:1838
  357.2 30.5 %collective-permute-start.11 = (bf16[1536,384]{1,0:T(8,128)(2,1)S(1)}, bf16[1536,384]{1,0:T(8,128)(2,1)S(1)}, u32[]{:S(2)}, u32[]{:S(2)}) collective-permute-start(bf16[1536,384]{1,0:T(8,128)(2,1)S(1)} %broadcast_select_fusion.1), channel_id=1, source_target_pairs={{0,2},{1,3},{2,0},{3,1},{4,6},{5,7},{6,4},{7,5},{8,10},{9,11},{10,... | collective-permute-start | bytes 3538952 | tf_op jit(solution)/shard_map/ppermute | solution.py:1841
  359.0 16.4 %copy-start.59 = (bf16[2,256,1536]{2,1,0:T(8,128)(2,1)S(1)}, bf16[2,256,1536]{2,1,0:T(8,128)(2,1)}, u32[]{:S(2)}) copy-start(bf16[2,256,1536]{2,1,0:T(8,128)(2,1)} %slice_select_fusion) | copy-start | bytes 4718596
  359.3 52.3 %collective-permute-start.9 = (bf16[1536,384]{1,0:T(8,128)(2,1)S(1)}, bf16[1536,384]{1,0:T(8,128)(2,1)S(1)}, u32[]{:S(2)}, u32[]{:S(2)}) collective-permute-start(bf16[1536,384]{1,0:T(8,128)(2,1)S(1)} %broadcast_select_fusion.2), channel_id=1, source_target_pairs={{0,2},{1,3},{2,0},{3,1},{4,6},{5,7},{6,4},{7,5},{8,10},{9,11},{10,... | collective-permute-start | bytes 3538952 | tf_op jit(solution)/shard_map/ppermute | solution.py:1841
  376.0 78.4 %collective-permute-start.2 = (bf16[256,1536]{1,0:T(8,128)(2,1)S(1)}, bf16[256,1536]{1,0:T(8,128)(2,1)S(1)}, u32[]{:S(2)}, u32[]{:S(2)}) collective-permute-start(bf16[256,1536]{1,0:T(8,128)(2,1)S(1)} %fusion.10), channel_id=1, source_target_pairs={{0,16},{16,0},{1,17},{17,1},{2,18},{18,2},{3,19},{19,3},{4,20},{20... | collective-permute-start | bytes 2359304 | tf_op jit(solution)/shard_map/ppermute | solution.py:1835
  413.1 3.8 copy-start.50
  413.1 4.3 copy-start.52
  414.2 25.0 %copy-start.53 = (bf16[4,384,896]{2,1,0:T(8,128)(2,1)}, bf16[4,384,896]{2,1,0:T(8,128)(2,1)S(1)}, u32[]{:S(2)}) copy-start(bf16[4,384,896]{2,1,0:T(8,128)(2,1)S(1)} %add_convert_fusion) | copy-start | bytes 8257540
  438.4 6.6 copy-start.45
  438.5 9.2 %copy-start.43 = (bf16[4,256,768]{2,1,0:T(8,128)(2,1)}, bf16[4,256,768]{2,1,0:T(8,128)(2,1)S(1)}, u32[]{:S(2)}) copy-start(bf16[4,256,768]{2,1,0:T(8,128)(2,1)S(1)} %get-tuple-element.100) | copy-start | bytes 4718596
  438.5 17.4 %copy-start.5 = (bf16[4,256,384]{2,1,0:T(8,128)(2,1)}, bf16[4,256,384]{2,1,0:T(8,128)(2,1)S(1)}, u32[]{:S(2)}) copy-start(bf16[4,256,384]{2,1,0:T(8,128)(2,1)S(1)} %get-tuple-element.101) | copy-start | bytes 2359300
  438.5 6.5 copy-start.64
  439.2 17.4 %collective-permute-start.6 = (bf16[1024,128]{1,0:T(8,128)(2,1)}, bf16[1024,128]{1,0:T(8,128)(2,1)}, u32[]{:S(2)}, u32[]{:S(2)}) collective-permute-start(bf16[1024,128]{1,0:T(8,128)(2,1)} %broadcast_select_fusion.11), channel_id=1, source_target_pairs={{0,16},{16,0},{1,17},{17,1},{2,18},{18,2},{3,19},{19,3},{4,20},{20... | collective-permute-start | bytes 786440 | tf_op jit(solution)/shard_map/ppermute | solution.py:1835
  440.6 38.6 %collective-permute-start.14 = (bf16[384,896]{1,0:T(8,128)(2,1)}, bf16[384,896]{1,0:T(8,128)(2,1)}, u32[]{:S(2)}, u32[]{:S(2)}) collective-permute-start(bf16[384,896]{1,0:T(8,128)(2,1)} %get-tuple-element.165), channel_id=1, source_target_pairs={{0,12},{4,0},{8,4},{12,8},{1,13},{5,1},{9,5},{13,9},{2,14},{6,2},{... | collective-permute-start | bytes 2064392 | tf_op jit(solution)/shard_map/ppermute | solution.py:1956
  444.2 55.6 %collective-permute-start.13 = (bf16[384,896]{1,0:T(8,128)(2,1)}, bf16[384,896]{1,0:T(8,128)(2,1)}, u32[]{:S(2)}, u32[]{:S(2)}) collective-permute-start(bf16[384,896]{1,0:T(8,128)(2,1)} %get-tuple-element.166), channel_id=1, source_target_pairs={{0,8},{4,12},{8,0},{12,4},{1,9},{5,13},{9,1},{13,5},{2,10},{6,14},... | collective-permute-start | bytes 2064392 | tf_op jit(solution)/shard_map/ppermute | solution.py:1956
  444.3 55.6 %collective-permute-start.12 = (bf16[384,896]{1,0:T(8,128)(2,1)}, bf16[384,896]{1,0:T(8,128)(2,1)}, u32[]{:S(2)}, u32[]{:S(2)}) collective-permute-start(bf16[384,896]{1,0:T(8,128)(2,1)} %get-tuple-element.164), channel_id=1, source_target_pairs={{0,4},{4,8},{8,12},{12,0},{1,5},{5,9},{9,13},{13,1},{2,6},{6,10},{... | collective-permute-start | bytes 2064392 | tf_op jit(solution)/shard_map/ppermute | solution.py:1956
  455.9 10.9 %copy-start.9 = (bf16[4,256,1536]{2,1,0:T(8,128)(2,1)S(1)}, bf16[4,256,1536]{2,1,0:T(8,128)(2,1)}, u32[]{:S(2)}) copy-start(bf16[4,256,1536]{2,1,0:T(8,128)(2,1)} %copy-done.7) | copy-start | bytes 9437188
  456.7 10.1 %copy-start.70 = (bf16[1024,64]{1,0:T(8,128)(2,1)S(1)}, bf16[1024,64]{1,0:T(8,128)(2,1)}, u32[]{:S(2)}) copy-start(bf16[1024,64]{1,0:T(8,128)(2,1)} %slice.371) | copy-start | bytes 393220
  458.4 8.3 %collective-permute-start.7 = (bf16[1024,64]{1,0:T(8,128)(2,1)S(1)}, bf16[1024,64]{1,0:T(8,128)(2,1)S(1)}, u32[]{:S(2)}, u32[]{:S(2)}) collective-permute-start(bf16[1024,64]{1,0:T(8,128)(2,1)S(1)} %broadcast_select_fusion.13), channel_id=1, source_target_pairs={{0,1},{1,0},{2,3},{3,2},{4,5},{5,4},{6,7},{7,6},{8,9},{9,8},{10,11... | collective-permute-start | bytes 393224 | tf_op jit(solution)/shard_map/ppermute | solution.py:1838
  466.8 5.4 copy-start.44
  476.2 23.7 %copy-start.54 = (bf16[4,384,896]{2,1,0:T(8,128)(2,1)S(1)}, bf16[4,384,896]{2,1,0:T(8,128)(2,1)}, u32[]{:S(2)}) copy-start(bf16[4,384,896]{2,1,0:T(8,128)(2,1)} %copy-done.53) | copy-start | bytes 8257540
  502.8 155.4 %copy-start.2 = (bf16[4,256,1536]{2,1,0:T(8,128)(2,1)S(1)}, bf16[4,256,1536]{2,1,0:T(8,128)(2,1)}, u32[]{:S(2)}) copy-start(bf16[4,256,1536]{2,1,0:T(8,128)(2,1)} %copy-done.1) | copy-start | bytes 9437188
  658.3 3.6 copy-start.6
  (40 other events, 78.9 us)
